TPU v7x, 16 devices: a whole 2x2x2 slice. The times are simulated.
16 devices in a mesh: tp: 2 (over z), sp: 8 (over y, x, core).
Axes of the slice: x: 2, y: 2, z: 2, core: 2. Of those that a mesh axis runs over, the one named last changes fastest.
Arguments:
- x_tok: bfloat16 [256, 5120], replicated
- seq_lens: int32 [256], replicated
- k_cache: bfloat16 [256, 256, 8, 128], P(None, 'sp', 'tp')
- v_cache: bfloat16 [256, 256, 8, 128], P(None, 'sp', 'tp')
- g_attn: bfloat16 [5120], replicated
- w_q: bfloat16 [5120, 4096], P(None, 'tp')
- w_k: bfloat16 [5120, 1024], P(None, 'tp')
- w_v: bfloat16 [5120, 1024], P(None, 'tp')
- w_o: bfloat16 [4096, 5120], P('tp')
- g_mlp: bfloat16 [5120], replicated
- w_gate: bfloat16 [5120, 14336], P(None, 'tp')
- w_up: bfloat16 [5120, 14336], P(None, 'tp')
- w_down: bfloat16 [14336, 5120], P('tp')
Outputs:
- output 1: bfloat16 [256, 5120], replicated
- output 2: bfloat16 [256, 256, 8, 128], P(None, 'sp', 'tp')
- output 3: bfloat16 [256, 256, 8, 128], P(None, 'sp', 'tp')
All inputs are finite; a program needn't handle non-finite values.
Results may differ from a plain program's by a relative error of at most 0.013755.
Values sent between devices are 32-bit elements.
A program may use at most 1.25 GiB of HBM per device.

v0:
```python
import jax
import jax.numpy as jnp
from jax import lax
from jax.sharding import PartitionSpec as P

ROPE_BASE = 500000.0
NORM_EPS = 1e-5


def rms_norm(x_in, norm_gain):
    x_f32 = x_in.astype(jnp.float32)
    inv_rms = lax.rsqrt(jnp.mean(x_f32 * x_f32, axis=-1, keepdims=True) + NORM_EPS)
    return (x_f32 * inv_rms * norm_gain.astype(jnp.float32)).astype(jnp.bfloat16)


def apply_rope(heads_in, positions):
    head_dim = heads_in.shape[-1]
    half_dim = head_dim // 2
    inv_freq = jnp.power(jnp.float32(ROPE_BASE), jnp.arange(half_dim, dtype=jnp.float32) * (-2.0 / head_dim))
    angles = positions.astype(jnp.float32)[:, None, None] * inv_freq
    cos_a = jnp.cos(angles)
    sin_a = jnp.sin(angles)
    heads_f32 = heads_in.astype(jnp.float32)
    first_half = heads_f32[..., :half_dim]
    second_half = heads_f32[..., half_dim:]
    rotated = jnp.concatenate([first_half * cos_a - second_half * sin_a, second_half * cos_a + first_half * sin_a], axis=-1)
    return rotated.astype(jnp.bfloat16)


def solution(mesh):
    cache_spec = P(None, "sp", "tp", None)
    col_spec = P(None, "tp")
    row_spec = P("tp", None)
    full_spec = P()

    def local_step(x_tok, seq_lens, k_blk, v_blk, g_attn, wq_loc, wk_loc, wv_loc, wo_loc, g_mlp, wg_loc, wu_loc, wd_loc):
        batch_rows, seq_blk, kv_loc, head_dim = k_blk.shape
        q_loc = wq_loc.shape[1] // head_dim
        groups = q_loc // kv_loc
        x_norm = rms_norm(x_tok, g_attn)
        q_new = jnp.dot(x_norm, wq_loc, preferred_element_type=jnp.float32).astype(jnp.bfloat16).reshape(batch_rows, q_loc, head_dim)
        k_new = jnp.dot(x_norm, wk_loc, preferred_element_type=jnp.float32).astype(jnp.bfloat16).reshape(batch_rows, kv_loc, head_dim)
        v_new = jnp.dot(x_norm, wv_loc, preferred_element_type=jnp.float32).astype(jnp.bfloat16).reshape(batch_rows, kv_loc, head_dim)
        q_rot = apply_rope(q_new, seq_lens)
        k_rot = apply_rope(k_new, seq_lens)
        local_pos = lax.axis_index("sp") * seq_blk + jnp.arange(seq_blk)
        is_new = (local_pos[None, :] == seq_lens[:, None])[:, :, None, None]
        k_out = jnp.where(is_new, k_rot[:, None], k_blk)
        v_out = jnp.where(is_new, v_new[:, None], v_blk)
        q_grp = q_rot.reshape(batch_rows, kv_loc, groups, head_dim)
        scores = jnp.einsum("bkgd,bskd->bkgs", q_grp, k_out, preferred_element_type=jnp.float32) * (head_dim ** -0.5)
        is_valid = (local_pos[None, :] <= seq_lens[:, None])[:, None, None, :]
        masked = jnp.where(is_valid, scores, -1e30)
        blk_max = jnp.max(masked, axis=-1, keepdims=True)
        weights = jnp.where(is_valid, jnp.exp(masked - blk_max), 0.0)
        blk_sum = jnp.sum(weights, axis=-1, keepdims=True)
        blk_mix = jnp.einsum("bkgs,bskd->bkgd", weights.astype(jnp.bfloat16), v_out, preferred_element_type=jnp.float32)
        glob_max = lax.pmax(blk_max, "sp")
        factor = jnp.exp(blk_max - glob_max)
        packed = lax.psum(jnp.concatenate([blk_mix * factor, blk_sum * factor], axis=-1), "sp")
        attn_out = (packed[..., :head_dim] / packed[..., head_dim:]).astype(jnp.bfloat16).reshape(batch_rows, q_loc * head_dim)
        attn_proj = lax.psum(jnp.dot(attn_out, wo_loc, preferred_element_type=jnp.float32), "tp")
        hidden = (x_tok.astype(jnp.float32) + attn_proj).astype(jnp.bfloat16)
        h_norm = rms_norm(hidden, g_mlp)
        gate_proj = jnp.dot(h_norm, wg_loc, preferred_element_type=jnp.float32).astype(jnp.bfloat16)
        up_proj = jnp.dot(h_norm, wu_loc, preferred_element_type=jnp.float32).astype(jnp.bfloat16)
        act_prod = (jax.nn.silu(gate_proj.astype(jnp.float32)) * up_proj.astype(jnp.float32)).astype(jnp.bfloat16)
        mlp_out = lax.psum(jnp.dot(act_prod, wd_loc, preferred_element_type=jnp.float32), "tp")
        y_out = (hidden.astype(jnp.float32) + mlp_out).astype(jnp.bfloat16)
        return y_out, k_out, v_out

    return jax.shard_map(local_step, mesh=mesh, in_specs=(full_spec, full_spec, cache_spec, cache_spec, full_spec, col_spec, col_spec, col_spec, row_spec, full_spec, col_spec, col_spec, row_spec), out_specs=(full_spec, cache_spec, cache_spec), check_vma=False)
```

profile of v0, /device:TPU:0, one launch (start us, length us, event | category | flops | bytes accessed | tf_op | source)
XLA Modules:
  0.0 565.7 jit_solution(9527830326322363886)
XLA Ops:
  7.2 0.0 all-reduce.4.cloned.1.call-start
  7.2 0.7 convert_element_type.85
  7.9 2.3 fusion.11
  10.3 0.7 convert_element_type.80
  11.0 0.8 broadcast_compare_fusion.1
  11.8 0.0 copy-start
  11.8 5.0 convolution_convert_fusion.3
  16.8 0.1 broadcast_in_dim.70
  16.9 0.0 copy-done
  16.9 4.8 fusion.27
  21.7 1.2 reshape.169
  22.9 10.2 %fusion.22 = f32[32,8,16,128]{3,1,2,0:T(8,128)S(1)} fusion(bf16[5120,2048]{1,0:T(8,128)(2,1)} %param.18, bf16[256,5120]{1,0:T(8,128)(2,1)S(1)} %copy-done, f32[5120]{0:T(1024)S(1)} %convert_element_type.80, f32[256]{0:T(256)S(1)} %add_rsqrt_fusion.1), kind=kOutput, calls=%fused_computation.41 | convolution fusion | flops 5375000576 | bytes 25711616 | tf_op jit(solution)/shard_map/dot_general | solution.py:41
  33.1 0.4 copy.48
  33.5 0.5 multiply_cosine_fusion
  34.1 0.5 subtract_convert_fusion.1
  34.6 2.1 subtract_convert_fusion
  36.7 0.4 pad_maximum_fusion.1
  37.0 13.9 %broadcast_select_fusion = (bf16[256,32,4,128]{3,2,1,0:T(4,128)(2,1)}, bf16[256,32,4,128]{3,2,1,0:T(4,128)(2,1)S(1)}) fusion(bf16[256,32,4,128]{3,2,1,0:T(4,128)(2,1)} %param.16, pred[256,32]{1,0:T(8,128)(4,1)S(1)} %get-tuple-element.14, bf16[256,4,128]{2,1,0:T(4,128)(2,1)S(1)} %broadcast_in_dim.70, bf16[256,32,4,128]{3,2,1,0:T(4,128)(2,1)} %param.15, ...), kind=kLoop, calls=%fused_computation.11 | loop fusion | flops 8388608 | bytes 34086912 | tf_op jit(solution)/shard_map/jit(_where)/select_n | solution.py:49
  50.9 0.0 copy-start.1
  51.0 9.5 %fusion.23 = (f32[256,4,4]{2,1,0:T(4,128)S(1)}, f32[256,4,4,32]{3,2,1,0:T(4,128)}) fusion(pred[256,32]{1,0:T(8,128)(4,1)S(1)} %get-tuple-element.13, bf16[256,32,4,128]{3,2,1,0:T(4,128)(2,1)S(1)} %get-tuple-element.12, bf16[256,4,4,64]{3,2,1,0:T(4,128)(2,1)} %bitcast.30, bf16[256,4,4,64]{3,2,1,0:T(4,128)(2,1)} %bitcast.29), kind=kOutput, calls=%fused_computation.42 | convolution fusion | flops 36040704 | bytes 9986048 | tf_op jit(solution)/shard_map/bkgd,bskd->bkgs/dot_general | solution.py:51
  60.4 0.0 copy-done.1
  60.4 0.2 copy.41
  60.6 26.5 %pmax.7 = f32[256,4,4,1]{0,2,3,1:T(4,128)S(1)} all-reduce(f32[256,4,4,1]{0,2,3,1:T(4,128)S(1)} %bitcast.31), channel_id=1, replica_groups=mesh['tp'=2,'sp'=8] {'sp'}, use_global_device_ids=true, to_apply=%region_2.3 | all-reduce | flops 4096 | bytes 32768 | tf_op jit(solution)/shard_map/pmax | solution.py:58
  87.1 7.2 %fusion.35 = f32[256,4,4]{2,1,0:T(4,128)S(1)} fusion(f32[256,4,4]{2,1,0:T(4,128)S(1)} %get-tuple-element.17, f32[256,4,4,32]{3,2,1,0:T(4,128)} %get-tuple-element.18, pred[256,32]{1,0:T(8,128)(4,1)S(1)} %get-tuple-element.13), kind=kLoop, calls=%fused_computation.51 | loop fusion | flops 651264 | bytes 565248 | tf_op jit(solution)/shard_map/reduce_sum | solution.py:56
  94.3 0.2 copy.43
  94.5 0.3 copy.42
  94.8 1.3 copy.44
  96.1 5.8 %fusion.24 = f32[256,4,4,128]{3,2,1,0:T(4,128)S(1)} fusion(bf16[256,32,4,128]{3,2,1,0:T(4,128)(2,1)} %get-tuple-element.11, f32[256,4,4]{2,1,0:T(4,128)S(1)} %copy.42, f32[256,4,4,32]{3,2,1,0:T(4,128)} %get-tuple-element.18, f32[256,4,4]{2,1,0:T(4,128)S(1)} %get-tuple-element.17, pred[256,32]{1,0:T(8,128)(4,1)S(1)} %get-tuple-element.13), kind=kOutput, calls=%fused_computation.43 | convolution fusion | flops 34734080 | bytes 11051008 | tf_op jit(solution)/shard_map/bkgs,bskd->bkgd/dot_general | solution.py:57
  101.9 3.2 pad_maximum_fusion
  105.1 0.0 all-reduce.4.cloned.1.call-update
  105.1 0.0 all-reduce.6.cloned.1.call-start
  105.2 72.2 %all-reduce.4.cloned.1.call-done = f32[256,4,4,129]{3,2,1,0:T(4,128)} async-done(((f32[256,4,4,129]{3,2,1,0:T(4,128)}), f32[256,4,4,129]{3,2,1,0:T(4,128)}) %all-reduce.4.cloned.1.call-update) | async-done | bytes 2113552 | tf_op jit(solution)/shard_map/psum | solution.py:60
  177.4 1.6 slice-done
  179.0 6.4 %copy.47 = f32[256,4,4,1]{2,1,0,3:T(4,128)S(1)} copy(f32[256,4,4,1]{3,2,1,0:T(4,128)S(1)} %slice-done) | data formatting | bytes 32768 | tf_op jit(solution)/shard_map/div | solution.py:61
  185.4 3.3 fusion.21
  188.7 0.8 reshape.167
  189.5 12.2 %fusion.46 = f32[256,5120]{1,0:T(8,128)} fusion(bf16[256,2048]{1,0:T(8,128)(2,1)S(1)} %reshape.167, bf16[2048,5120]{1,0:T(8,128)(2,1)} %param.21), kind=kOutput, calls=%fused_computation.71 | convolution fusion | flops 5368709120 | bytes 27262976 | tf_op jit(solution)/shard_map/dot_general | solution.py:62
  201.8 0.0 all-reduce.6.cloned.1.call-update
  201.8 0.0 all-reduce.8.cloned.1.call-start
  201.8 0.6 copy-done.2
  202.5 126.1 %all-reduce.6.cloned.1.call-done = f32[256,5120]{1,0:T(8,128)} async-done(((f32[256,5120]{1,0:T(8,128)}), f32[256,5120]{1,0:T(8,128)}) %all-reduce.6.cloned.1.call-update) | async-done | bytes 5242896 | tf_op jit(solution)/shard_map/psum | solution.py:62
  328.6 4.3 fusion.15
  332.9 30.5 %convolution_convert_fusion.1 = bf16[256,7168]{1,0:T(8,128)(2,1)} fusion(bf16[5120,7168]{1,0:T(8,128)(2,1)} %param.23, bf16[256,5120]{1,0:T(8,128)(2,1)S(1)} %get-tuple-element.4, f32[5120]{0:T(1024)S(1)} %convert_element_type.94, f32[256]{0:T(256)S(1)} %add_rsqrt_fusion), kind=kOutput, calls=%fused_computation.6 | convolution fusion | flops 18797559808 | bytes 79713280 | tf_op jit(solution)/shard_map/dot_general | solution.py:65
  363.5 32.5 %fusion.2.clone.4 = bf16[256,7168]{1,0:T(8,128)(2,1)} fusion(bf16[5120,7168]{1,0:T(8,128)(2,1)} %param.24, bf16[256,7168]{1,0:T(8,128)(2,1)} %convolution_convert_fusion.1, bf16[256,5120]{1,0:T(8,128)(2,1)S(1)} %get-tuple-element.4, f32[5120]{0:T(1024)S(1)} %convert_element_type.94, f32[256]{0:T(256)S(1)} %add_rsqrt_fusion), kind=kOutput, calls=%fused_computation.5.clone.clone.clone.1 | convolution fusion | flops 18812239872 | bytes 83383296 | tf_op jit(solution)/shard_map/dot_general | solution.py:66
  395.9 31.7 %fusion.10 = f32[256,5120]{1,0:T(8,128)} fusion(bf16[7168,5120]{1,0:T(8,128)(2,1)} %param.25, bf16[256,7168]{1,0:T(8,128)(2,1)} %fusion.2.clone.4), kind=kOutput, calls=%fused_computation.22 | convolution fusion | flops 18790481920 | bytes 82313216 | tf_op jit(solution)/shard_map/dot_general | solution.py:68
  427.6 0.0 all-reduce.8.cloned.1.call-update
  427.6 126.7 %all-reduce.8.cloned.1.call-done = f32[256,5120]{1,0:T(8,128)} async-done(((f32[256,5120]{1,0:T(8,128)}), f32[256,5120]{1,0:T(8,128)}) %all-reduce.8.cloned.1.call-update) | async-done | bytes 5242896 | tf_op jit(solution)/shard_map/psum | solution.py:68
  554.3 4.7 fusion.18
  (8 shorter events, 0.1 us)
Async XLA Ops:
  7.2 170.2 %all-reduce.4.cloned.1.call-start = ((), (), s32[]{:S(2)}) async-start(), calls=%async_computation | async-start | bytes 8388608 | tf_op jit(solution)/shard_map/psum | solution.py:60
  11.8 5.1 copy-start
  50.9 9.5 %copy-start.1 = (bf16[256,32,4,128]{3,2,1,0:T(4,128)(2,1)}, bf16[256,32,4,128]{3,2,1,0:T(4,128)(2,1)S(1)}, u32[]{:S(2)}) copy-start(bf16[256,32,4,128]{3,2,1,0:T(4,128)(2,1)S(1)} %get-tuple-element.12) | copy-start | bytes 25165828
  105.1 223.5 %all-reduce.6.cloned.1.call-start = ((), (), s32[]{:S(2)}) async-start(), calls=%async_computation.1 | async-start | bytes 10485760 | tf_op jit(solution)/shard_map/psum | solution.py:62
  177.4 1.6 slice-start
  201.8 0.7 copy-start.2
  201.8 352.5 %all-reduce.8.cloned.1.call-start = ((), (), s32[]{:S(2)}) async-start(), calls=%async_computation.2 | async-start | bytes 10485760 | tf_op jit(solution)/shard_map/psum | solution.py:68
Sparse Core Ops, SparseCore 0:
  105.2 72.1 all-reduce.3
  201.9 126.6 all-reduce.5
  427.7 126.5 all-reduce.7
where the time goes:
time: 570 us; the launch traced here: 566 us
  waiting for transfers between devices  325 us (57%)
  matrix products  142 us (25%)
  other arithmetic  44.6 us (8%)
  blocking collectives  26.5 us (5%)
  between operations  14.2 us (2%)
  local copies, waits for them, and re-layouts  13.1 us (2%)
    psum x1, waiting for transfers between devices, local_step(): lax.psum(jnp.dot(act_prod, wd_loc, preferred_element_type=jnp.float32), '...  127 us
    psum x1, waiting for transfers between devices, local_step(): lax.psum(jnp.dot(attn_out, wo_loc, preferred_element_type=jnp.float32), '...  126 us
    psum x1, waiting for transfers between devices, local_step(): lax.psum(jnp.concatenate([blk_mix * factor, blk_sum * factor], axis=-1),...  72.2 us
    dot_general x1, matrix products, local_step(): jnp.dot(h_norm, wu_loc, preferred_element_type=jnp.float32)  32.5 us
    dot_general x1, matrix products, local_step(): jnp.dot(act_prod, wd_loc, preferred_element_type=jnp.float32)  31.7 us
    dot_general x1, matrix products, local_step(): jnp.dot(h_norm, wg_loc, preferred_element_type=jnp.float32)  30.5 us
    pmax x1, blocking collectives, local_step(): glob_max = lax.pmax(blk_max, 'sp')  26.5 us
    select_n x1, other arithmetic, local_step(): v_out = jnp.where(is_new, v_new[:, None], v_blk)  13.9 us
  transfers between devices with their start and end apart: 3, of which 3 were waited for; matrix products, arithmetic and copies ran while one was open for 0% of the time, Pallas kernels for 0%

commit v1 on v0

v1 whole, which is shorter than its diff:
```python
import functools

import jax
import jax.numpy as jnp
from jax import lax
from jax.experimental import pallas as pl
from jax.experimental.pallas import tpu as pltpu
from jax.sharding import PartitionSpec as P

ROPE_BASE = 500000.0
NORM_EPS = 1e-5
MESH = pl.DeviceIdType.MESH
VMEM_LIMIT = 60 * 1024 * 1024


def qkv_kernel(x_ref, g_ref, cos_ref, sin_ref, wq_ref, wk_ref, wv_ref, out_ref, u_ref, *, nq, nk):
    i = pl.program_id(0)

    @pl.when(i == 0)
    def _():
        xf = x_ref[...].astype(jnp.float32)
        inv = lax.rsqrt(jnp.mean(xf * xf, axis=-1, keepdims=True) + NORM_EPS)
        u_ref[...] = (xf * inv * g_ref[...].astype(jnp.float32)).astype(jnp.bfloat16)

    def project(w_ref, rope):
        y = jnp.dot(u_ref[...], w_ref[...], preferred_element_type=jnp.float32)
        y = y.astype(jnp.bfloat16)
        if rope:
            for h in range(y.shape[1] // 128):
                t = y[:, h * 128 : (h + 1) * 128].astype(jnp.float32)
                r = t * cos_ref[...] + pltpu.roll(t, 64, 1) * sin_ref[...]
                out_ref[:, h * 128 : (h + 1) * 128] = r.astype(jnp.bfloat16)
        else:
            out_ref[...] = y

    @pl.when(i < nq)
    def _():
        project(wq_ref, True)

    @pl.when(jnp.logical_and(i >= nq, i < nq + nk))
    def _():
        project(wk_ref, True)

    @pl.when(i >= nq + nk)
    def _():
        project(wv_ref, False)


def qkv_call(x_tok, g_attn, cos_f, sin_f, wq, wk, wv):
    rows, dim = x_tok.shape
    bn = 256
    nq, nk, nv = wq.shape[1] // bn, wk.shape[1] // bn, wv.shape[1] // bn
    whole = lambda i: (0, 0)
    return pl.pallas_call(
        functools.partial(qkv_kernel, nq=nq, nk=nk),
        grid=(nq + nk + nv,),
        in_specs=[
            pl.BlockSpec((rows, dim), whole),
            pl.BlockSpec((1, dim), whole),
            pl.BlockSpec((rows, 128), whole),
            pl.BlockSpec((rows, 128), whole),
            pl.BlockSpec((dim, bn), lambda i: (0, jnp.minimum(i, nq - 1))),
            pl.BlockSpec((dim, bn), lambda i: (0, jnp.clip(i - nq, 0, nk - 1))),
            pl.BlockSpec((dim, bn), lambda i: (0, jnp.clip(i - nq - nk, 0, nv - 1))),
        ],
        out_specs=pl.BlockSpec((rows, bn), lambda i: (0, i)),
        out_shape=jax.ShapeDtypeStruct((rows, (nq + nk + nv) * bn), jnp.bfloat16),
        scratch_shapes=[pltpu.VMEM((rows, dim), jnp.bfloat16)],
        compiler_params=pltpu.CompilerParams(vmem_limit_bytes=VMEM_LIMIT),
        name="qkv",
    )(x_tok, g_attn.reshape(1, dim), cos_f, sin_f, wq, wk, wv)


PAIRS = 8


def att_kernel(lens_ref, base_ref, q_ref, kn_ref, vn_ref, k_ref, v_ref, ko_ref, vo_ref, mix_ref, m_ref, l_ref):
    step = pl.program_id(0)
    base = base_ref[0]

    @pl.when(step == 0)
    def _():
        m_ref[...] = jnp.zeros_like(m_ref)
        l_ref[...] = jnp.zeros_like(l_ref)

    row = lax.broadcasted_iota(jnp.int32, (128, 128), 0)
    row_pos = base + row // 4
    ri = lax.broadcasted_iota(jnp.int32, (32, 256), 0)
    ci = lax.broadcasted_iota(jnp.int32, (32, 256), 1)
    same = jnp.logical_and(ri // 16 == ci // 128, (ri % 16) // 4 == ci % 4)
    col_pos = jnp.where(same, base + (ci % 128) // 4, 1 << 30)
    first = ri < 16
    lane = lax.broadcasted_iota(jnp.int32, (32, 128), 1)
    scale = 128.0 ** -0.5
    m_all, l_all = m_ref[...], l_ref[...]
    for j in range(PAIRS):
        pair = step * PAIRS + j
        p0 = lens_ref[2 * pair]
        p1 = lens_ref[2 * pair + 1]
        ks, vs = [], []
        for t, p in ((0, p0), (1, p1)):
            b = 2 * j + t
            hit = row_pos == p
            for src, new, dst, acc in ((k_ref, kn_ref, ko_ref, ks), (v_ref, vn_ref, vo_ref, vs)):
                old = src[b].astype(jnp.float32)
                add = jnp.broadcast_to(new[b][None], (16, 8, 128)).reshape(128, 128)
                val = jnp.where(hit, add, old).astype(jnp.bfloat16)
                dst[b] = val
                acc.append(val)
        kk = jnp.concatenate(ks, axis=0)
        vv = jnp.concatenate(vs, axis=0)
        s = lax.dot_general(q_ref[j], kk, (((1,), (1,)), ((), ())), preferred_element_type=jnp.float32) * scale
        valid = col_pos <= jnp.where(first, p0, p1)
        s = jnp.where(valid, s, -1e30)
        m = jnp.max(s, axis=1, keepdims=True)
        w = jnp.where(valid, jnp.exp(s - m), 0.0)
        l = jnp.sum(w, axis=1, keepdims=True)
        mix_ref[j] = jnp.dot(w.astype(jnp.bfloat16), vv, preferred_element_type=jnp.float32)
        m_all = jnp.where(lane == pair, m, m_all)
        l_all = jnp.where(lane == pair, l, l_all)
    m_ref[...] = m_all
    l_ref[...] = l_all


def att_call(seq_lens, base, q, kn, vn, k2, v2):
    batch = k2.shape[0]
    nb = 2 * PAIRS
    blk = lambda i, *_: (i, 0, 0)
    grid_spec = pltpu.PrefetchScalarGridSpec(
        num_scalar_prefetch=2,
        grid=(batch // nb,),
        in_specs=[
            pl.BlockSpec((PAIRS, 32, 128), blk),
            pl.BlockSpec((nb, 8, 128), blk),
            pl.BlockSpec((nb, 8, 128), blk),
            pl.BlockSpec((nb, 128, 128), blk),
            pl.BlockSpec((nb, 128, 128), blk),
        ],
        out_specs=[
            pl.BlockSpec((nb, 128, 128), blk),
            pl.BlockSpec((nb, 128, 128), blk),
            pl.BlockSpec((PAIRS, 32, 128), blk),
            pl.BlockSpec((32, 128), lambda i, *_: (0, 0)),
            pl.BlockSpec((32, 128), lambda i, *_: (0, 0)),
        ],
    )
    return pl.pallas_call(
        att_kernel,
        grid_spec=grid_spec,
        out_shape=[
            jax.ShapeDtypeStruct(k2.shape, jnp.bfloat16),
            jax.ShapeDtypeStruct(v2.shape, jnp.bfloat16),
            jax.ShapeDtypeStruct((batch // 2, 32, 128), jnp.float32),
            jax.ShapeDtypeStruct((32, 128), jnp.float32),
            jax.ShapeDtypeStruct((32, 128), jnp.float32),
        ],
        compiler_params=pltpu.CompilerParams(vmem_limit_bytes=VMEM_LIMIT),
        name="att",
    )(seq_lens, base, q, kn, vn, k2, v2)


def coords():
    z = lax.axis_index("tp")
    sp = lax.axis_index("sp")
    return z, sp // 4, (sp // 2) % 2, sp % 2


def device(z, y, x, c):
    return (z, y * 4 + x * 2 + c)


def flip(a, on):
    return 1 - a if on else a


def greet(peers):
    barrier = pltpu.get_barrier_semaphore()
    for p in peers:
        pl.semaphore_signal(barrier, inc=1, device_id=p, device_id_type=MESH)
    pl.semaphore_wait(barrier, len(peers))


def remote(src, dst, send, recv, dev):
    return pltpu.make_async_remote_copy(src_ref=src, dst_ref=dst, send_sem=send, recv_sem=recv, device_id=dev, device_id_type=MESH)


def combine_kernel(mix_ref, m_ref, l_ref, o_ref, got1, st_own, st1, comb, stc, got2, st2, s1, r1, s2, r2):
    z, y, x, c = coords()
    partner = device(z, y, x, 1 - c)
    chips = [(y, x), (y, 1 - x), (1 - y, x), (1 - y, 1 - x)]
    greet([partner] + [device(z, b, a, c) for b, a in chips[1:]])

    st_own[0] = m_ref[...]
    st_own[1] = l_ref[...]
    first = []
    for k in (1, 2, 3, 0):
        b, a = chips[k]
        start = 16 * (b * 4 + a * 2 + 1 - c)
        first.append(remote(mix_ref.at[pl.ds(start, 16)], got1.at[k], s1.at[k], r1.at[k], partner))
    stat1 = remote(st_own, st1, s1.at[4], r1.at[4], partner)
    stat1.start()
    for cp in first:
        cp.start()
    stat1.wait_recv()
    ma, mb = st_own[0], st1[0]
    mg = jnp.maximum(ma, mb)
    fa, fb = jnp.exp(ma - mg), jnp.exp(mb - mg)
    stc[0] = mg
    stc[1] = st_own[1] * fa + st1[1] * fb
    second = {}
    stats2 = {}
    for k in (1, 2, 3):
        b, a = chips[k]
        stats2[k] = remote(stc, st2.at[k - 1], s2.at[3 + k - 1], r2.at[3 + k - 1], device(z, b, a, c))
        stats2[k].start()
    for n, k in enumerate((1, 2, 3, 0)):
        b, a = chips[k]
        block = b * 4 + a * 2 + c
        back = (128 - 16 * block) % 128
        ga, gb = pltpu.roll(fa, back, 1), pltpu.roll(fb, back, 1)
        first[n].wait_recv()
        for j in range(16):
            comb[k, j] = mix_ref[16 * block + j] * ga[:, j : j + 1] + got1[k, j] * gb[:, j : j + 1]
        if k:
            second[k] = remote(comb.at[k], got2.at[k - 1], s2.at[k - 1], r2.at[k - 1], device(z, b, a, c))
            second[k].start()
    for k in (1, 2, 3):
        stats2[k].wait_recv()
    ms = [stc[0]] + [st2[k, 0] for k in range(3)]
    ls = [stc[1]] + [st2[k, 1] for k in range(3)]
    mg = jnp.maximum(jnp.maximum(ms[0], ms[1]), jnp.maximum(ms[2], ms[3]))
    fs = [jnp.exp(m - mg) for m in ms]
    total = ls[0] * fs[0] + ls[1] * fs[1] + ls[2] * fs[2] + ls[3] * fs[3]
    block = y * 4 + x * 2 + c
    back = (128 - 16 * block) % 128
    fs = [pltpu.roll(f, back, 1) for f in fs]
    total = pltpu.roll(total, back, 1)
    for k in (1, 2, 3):
        second[k].wait_recv()
    for j in range(16):
        acc = comb[0, j] * fs[0][:, j : j + 1]
        for k in (1, 2, 3):
            acc = acc + got2[k - 1, j] * fs[k][:, j : j + 1]
        o_ref[j] = (acc / total[:, j : j + 1]).astype(jnp.bfloat16)
    for cp in first + [stat1] + [stats2[k] for k in stats2] + [second[k] for k in second]:
        cp.wait_send()


def combine_call(mix, m, l):
    vm = pl.BlockSpec(memory_space=pltpu.VMEM)
    f32 = jnp.float32
    return pl.pallas_call(
        combine_kernel,
        out_shape=jax.ShapeDtypeStruct((16, 32, 128), jnp.bfloat16),
        in_specs=[vm, vm, vm],
        out_specs=vm,
        scratch_shapes=[
            pltpu.VMEM((4, 16, 32, 128), f32),
            pltpu.VMEM((2, 32, 128), f32),
            pltpu.VMEM((2, 32, 128), f32),
            pltpu.VMEM((4, 16, 32, 128), f32),
            pltpu.VMEM((2, 32, 128), f32),
            pltpu.VMEM((3, 16, 32, 128), f32),
            pltpu.VMEM((3, 2, 32, 128), f32),
            pltpu.SemaphoreType.DMA((5,)),
            pltpu.SemaphoreType.DMA((5,)),
            pltpu.SemaphoreType.DMA((6,)),
            pltpu.SemaphoreType.DMA((6,)),
        ],
        compiler_params=pltpu.CompilerParams(collective_id=0, has_side_effects=True, vmem_limit_bytes=VMEM_LIMIT),
        name="combine",
    )(mix, m, l)


def hidden_kernel(part_ref, x_ref, g_ref, h_ref, hid_ref, zb, hbuf, sz, rz, ss, rs, sd, rd):
    z, y, x, c = coords()
    partner = device(z, y, x, 1 - c)
    zdev = device(1 - z, y, x, c)
    z1, x1 = z + c * (1 - 2 * z), x + (1 - c) * (1 - 2 * x)
    z2, x2 = z + (1 - c) * (1 - 2 * z), x + c * (1 - 2 * x)
    dev1, dev2 = device(z1, y, x1, c), device(z2, y, x2, c)
    greet([partner, dev1, dev2])
    cz = remote(part_ref.at[pl.ds(16 * (1 - z), 16)], zb, sz, rz, zdev)
    cz.start()
    cz.wait_recv()
    own = part_ref[pl.ds(pl.multiple_of(16 * z, 16), 16), :]
    hid = (x_ref[...].astype(jnp.float32) + (own + zb[...])).astype(jnp.bfloat16).astype(jnp.float32)
    hid_ref[...] = hid
    inv = lax.rsqrt(jnp.mean(hid * hid, axis=-1, keepdims=True) + NORM_EPS)
    slot = lambda zz, xx, cc: (xx * 2 + cc) * 2 + zz
    mine = slot(z, x, c)
    hbuf[mine] = (hid * inv * g_ref[...].astype(jnp.float32)).astype(jnp.bfloat16).astype(jnp.float32)

    def send(sl, dev, s, r, n):
        cp = remote(hbuf.at[sl], hbuf.at[sl], s.at[n], r.at[n], dev)
        cp.start()
        return cp

    a1 = send(mine, dev1, ss, rs, 0)
    a2 = send(mine, dev2, ss, rs, 1)
    d0 = send(mine, partner, sd, rd, 0)
    a1.wait_recv()
    s1 = slot(z1, x1, c)
    a3 = send(s1, dev2, ss, rs, 2)
    d1 = send(s1, partner, sd, rd, 1)
    a2.wait_recv()
    d2 = send(slot(z2, x2, c), partner, sd, rd, 2)
    a3.wait_recv()
    d3 = send(slot(1 - z, 1 - x, c), partner, sd, rd, 3)
    for cp in (d0, d1, d2, d3):
        cp.wait_recv()
    for k in range(8):
        h_ref[pl.ds(16 * k, 16), :] = hbuf[k].astype(jnp.bfloat16)
    for cp in (cz, a1, a2, a3, d0, d1, d2, d3):
        cp.wait_send()


def hidden_call(part, xs, g):
    vm = pl.BlockSpec(memory_space=pltpu.VMEM)
    f32 = jnp.float32
    dim = part.shape[1]
    dma = pltpu.SemaphoreType.DMA
    return pl.pallas_call(
        hidden_kernel,
        out_shape=[jax.ShapeDtypeStruct((128, dim), jnp.bfloat16), jax.ShapeDtypeStruct((16, dim), f32)],
        in_specs=[vm, vm, vm],
        out_specs=[vm, vm],
        scratch_shapes=[
            pltpu.VMEM((16, dim), f32),
            pltpu.VMEM((8, 16, dim), f32),
            dma, dma, dma((3,)), dma((3,)), dma((4,)), dma((4,)),
        ],
        compiler_params=pltpu.CompilerParams(collective_id=1, has_side_effects=True, vmem_limit_bytes=VMEM_LIMIT),
        name="hidden",
    )(part, xs, g.reshape(1, dim))


def gate_up_kernel(idx_ref, h_ref, wg_ref, wu_ref, m_ref):
    g = jnp.dot(h_ref[...], wg_ref[...], preferred_element_type=jnp.float32).astype(jnp.bfloat16).astype(jnp.float32)
    u = jnp.dot(h_ref[...], wu_ref[...], preferred_element_type=jnp.float32).astype(jnp.bfloat16).astype(jnp.float32)
    m_ref[...] = (jax.nn.silu(g) * u).astype(jnp.bfloat16)


def gate_up_call(idx, h, wg, wu, ways):
    rows, dim = h.shape
    bn = 256
    steps = wg.shape[1] // ways // bn
    wspec = pl.BlockSpec((dim, bn), lambda i, s: (0, s[0] * steps + i))
    return pl.pallas_call(
        gate_up_kernel,
        grid_spec=pltpu.PrefetchScalarGridSpec(
            num_scalar_prefetch=1,
            grid=(steps,),
            in_specs=[pl.BlockSpec((rows, dim), lambda i, s: (0, 0)), wspec, wspec],
            out_specs=pl.BlockSpec((rows, bn), lambda i, s: (0, i)),
        ),
        out_shape=jax.ShapeDtypeStruct((rows, steps * bn), jnp.bfloat16),
        compiler_params=pltpu.CompilerParams(vmem_limit_bytes=VMEM_LIMIT),
        name="gate_up",
    )(idx, h, wg, wu)


def down_kernel(idx_ref, m_ref, wd_ref, o_ref):
    o_ref[...] = jnp.dot(m_ref[...], wd_ref[...], preferred_element_type=jnp.float32)


def down_call(idx, m, wd):
    rows, depth = m.shape
    bn = 512
    return pl.pallas_call(
        down_kernel,
        grid_spec=pltpu.PrefetchScalarGridSpec(
            num_scalar_prefetch=1,
            grid=(wd.shape[1] // bn,),
            in_specs=[pl.BlockSpec((rows, depth), lambda i, s: (0, 0)), pl.BlockSpec((depth, bn), lambda i, s: (s[0], i))],
            out_specs=pl.BlockSpec((rows, bn), lambda i, s: (0, i)),
        ),
        out_shape=jax.ShapeDtypeStruct((rows, wd.shape[1]), jnp.float32),
        compiler_params=pltpu.CompilerParams(vmem_limit_bytes=VMEM_LIMIT),
        name="down",
    )(idx, m, wd)


COLORS = ((0, 1664), (1664, 1664), (3328, 1792))


def output_kernel(part_ref, hid_ref, y_ref, got1, acc, got2, ybuf, s1, r1, s2, r2, sl, rl, sd, rd):
    z, y, x, c = coords()
    partner = device(z, y, x, 1 - c)
    chips = [(z, x), (z, 1 - x), (1 - z, x), (1 - z, 1 - x)]
    near = [device(z, y, 1 - x, c), device(z, 1 - y, x, c), device(1 - z, y, x, c)]
    greet([partner] + near + [device(1 - z, y, 1 - x, c)])
    slot = lambda zz, xx, cc: (xx * 2 + cc) * 2 + zz
    rows16 = lambda s: pl.ds(pl.multiple_of(16 * s, 16), 16)
    order = (3, 1, 2, 0)
    first = {}
    for k in order:
        zz, xx = chips[k]
        first[k] = remote(part_ref.at[rows16(slot(zz, xx, 1 - c))], got1.at[k], s1.at[k], r1.at[k], partner)
        first[k].start()
    second = {}
    for k in order:
        zz, xx = chips[k]
        first[k].wait_recv()
        acc[k] = part_ref[rows16(slot(zz, xx, c)), :] + got1[k]
        if k:
            second[k] = remote(acc.at[k], got2.at[k - 1], s2.at[k - 1], r2.at[k - 1], device(zz, y, xx, c))
            second[k].start()
    for k in (1, 2, 3):
        second[k].wait_recv()
    total = (acc[0] + got2[0]) + (got2[1] + got2[2])
    mine = y * 8 + slot(z, x, c)
    ybuf[mine] = (hid_ref[...] + total).astype(jnp.bfloat16).astype(jnp.float32)

    def shard(mask):
        zz, yy, xx = flip(z, mask & 4), flip(y, mask & 2), flip(x, mask & 1)
        return yy * 8 + slot(zz, xx, c)

    links, locals_ = {}, {}

    def piece(mask, k):
        return ybuf.at[shard(mask), :, pl.ds(*COLORS[k])]

    def push(mask, k, dim):
        n = 7 * k + (mask | (1 << dim)) - 1
        cp = remote(piece(mask, k), piece(mask, k), sl.at[n], rl.at[n], near[dim])
        cp.start()
        links[k, mask | (1 << dim)] = cp

    def across(mask, k):
        n = 8 * k + mask
        cp = remote(piece(mask, k), piece(mask, k), sd.at[n], rd.at[n], partner)
        cp.start()
        locals_[k, mask] = cp

    turn = lambda k: [(k + i) % 3 for i in range(3)]
    for i in range(3):
        for k in range(3):
            push(0, k, turn(k)[i])
    for k in range(3):
        across(0, k)
    for level in ((0,), (1,), (0, 1), (2,), (0, 2), (1, 2), (0, 1, 2)):
        for k in range(3):
            dims = turn(k)
            mask = sum(1 << dims[i] for i in level)
            links[k, mask].wait_recv()
            for i in range(max(level) + 1, 3):
                push(mask, k, dims[i])
            across(mask, k)
    for cp in locals_.values():
        cp.wait_recv()
    for s in range(16):
        y_ref[pl.ds(16 * s, 16), :] = ybuf[s].astype(jnp.bfloat16)
    for cp in list(first.values()) + list(second.values()) + list(links.values()) + list(locals_.values()):
        cp.wait_send()


def output_call(part, hid):
    vm = pl.BlockSpec(memory_space=pltpu.VMEM)
    f32 = jnp.float32
    dim = part.shape[1]
    dma = pltpu.SemaphoreType.DMA
    return pl.pallas_call(
        output_kernel,
        out_shape=jax.ShapeDtypeStruct((256, dim), jnp.bfloat16),
        in_specs=[vm, vm],
        out_specs=vm,
        scratch_shapes=[
            pltpu.VMEM((4, 16, dim), f32),
            pltpu.VMEM((4, 16, dim), f32),
            pltpu.VMEM((3, 16, dim), f32),
            pltpu.VMEM((16, 16, dim), f32),
            dma((4,)), dma((4,)), dma((3,)), dma((3,)), dma((21,)), dma((21,)), dma((24,)), dma((24,)),
        ],
        compiler_params=pltpu.CompilerParams(collective_id=2, has_side_effects=True, vmem_limit_bytes=VMEM_LIMIT),
        name="output",
    )(part, hid)


def solution(mesh):
    cache_spec = P(None, "sp", "tp", None)
    col_spec = P(None, "tp")
    row_spec = P("tp", None)
    full_spec = P()

    def local_step(x_tok, seq_lens, k_blk, v_blk, g_attn, wq_loc, wk_loc, wv_loc, wo_loc, g_mlp, wg_loc, wu_loc, wd_loc):
        batch, seq_blk, kv_loc, head_dim = k_blk.shape
        q_loc = wq_loc.shape[1] // head_dim
        half = head_dim // 2
        z, sp = lax.axis_index("tp"), lax.axis_index("sp")
        inv_freq = jnp.power(jnp.float32(ROPE_BASE), jnp.arange(half, dtype=jnp.float32) * (-2.0 / head_dim))
        angles = seq_lens.astype(jnp.float32)[:, None] * inv_freq
        cos_a, sin_a = jnp.cos(angles), jnp.sin(angles)
        cos_f = jnp.concatenate([cos_a, cos_a], axis=-1)
        sin_f = jnp.concatenate([-sin_a, sin_a], axis=-1)
        qkv = qkv_call(x_tok, g_attn, cos_f, sin_f, wq_loc, wk_loc, wv_loc)
        qw, kw = q_loc * head_dim, kv_loc * head_dim
        q = qkv[:, :qw].reshape(batch // 2, 2 * q_loc, head_dim)
        twice = lambda t: jnp.concatenate([t, t], axis=1).astype(jnp.float32)
        kn = twice(qkv[:, qw : qw + kw].reshape(batch, kv_loc, head_dim))
        vn = twice(qkv[:, qw + kw :].reshape(batch, kv_loc, head_dim))
        base = (sp * seq_blk).astype(jnp.int32).reshape(1)
        flat = (batch, seq_blk * kv_loc, head_dim)
        k_out, v_out, mix, m, l = att_call(seq_lens, base, q, kn, vn, k_blk.reshape(flat), v_blk.reshape(flat))
        o = combine_call(mix, m, l).reshape(32, q_loc * head_dim)
        part = jnp.dot(o, wo_loc, preferred_element_type=jnp.float32)
        xs = lax.dynamic_slice_in_dim(x_tok, 32 * sp + 16 * z, 16, 0)
        h, hid = hidden_call(part, xs, g_mlp)
        idx = (sp % 4).astype(jnp.int32).reshape(1)
        act = gate_up_call(idx, h, wg_loc, wu_loc, 4)
        down = down_call(idx, act, wd_loc)
        y_out = output_call(down, hid)
        return y_out, k_out.reshape(k_blk.shape), v_out.reshape(v_blk.shape)

    return jax.shard_map(local_step, mesh=mesh, in_specs=(full_spec, full_spec, cache_spec, cache_spec, full_spec, col_spec, col_spec, col_spec, row_spec, full_spec, col_spec, col_spec, row_spec), out_specs=(full_spec, cache_spec, cache_spec), check_vma=False)
```

time: 570 us -> 208 us (0.36)
  waiting for transfers between devices: 325 us -> 0 us
  Pallas kernels: 0 us -> 180 us
  matrix products: 142 us -> 9.71 us
  other arithmetic: 44.6 us -> 4.48 us
  blocking collectives: 26.5 us -> 0 us
  between operations: 14.2 us -> 0.71 us
    psum x3 -> x0, waiting for transfers between devices: 325 us -> none  [the longest x1 127 us: local_step(): lax.psum(jnp.dot(act_prod, wd_loc, preferred_element_type=jnp.float32), '...]
    pallas_call x0 -> x7, Pallas kernels: none -> 180 us  [the longest x1 42.9 us: output_call(): pl.pallas_call(output_kernel, out_shape=jax.ShapeDtypeStruct((256, dim),...]
    dot_general x9 -> x1, matrix products: 142 us -> 9.71 us  [local_step(): part = jnp.dot(o, wo_loc, preferred_element_type=jnp.float32)]
    pmax x1 -> x0, blocking collectives: 26.5 us -> none  [local_step(): glob_max = lax.pmax(blk_max, 'sp')]
    select_n x1 -> x0, other arithmetic: 13.9 us -> none  [local_step(): v_out = jnp.where(is_new, v_new[:, None], v_blk)]
    reduce_sum x3 -> x0, other arithmetic: 13.9 us -> none  [the longest x1 7.18 us: local_step(): blk_sum = jnp.sum(weights, axis=-1, keepdims=True)]
    div x1 -> x0, local copies, waits for them, and re-layouts: 6.45 us -> none  [local_step(): packed[..., :head_dim] / packed[..., head_dim:]]
    convert_element_type x5 -> x3, other arithmetic: 9.31 us -> 3.1 us  [the longest x2 2.42 us: local_step(): twice = lambda t: jnp.concatenate([t, t], axis=1).astype(jnp.float32)]
  transfers between devices with their start and end apart: 3 -> 0, of which waited for: 3 -> 0; matrix products, arithmetic and copies ran while one was open for 0% -> 0% of each run, Pallas kernels for 0% -> 0%
where the time goes in v1:
time: 208 us; the launch traced here: 207 us
  Pallas kernels  180 us (87%)
  local copies, waits for them, and re-layouts  12.4 us (6%)
  matrix products  9.71 us (5%)
  other arithmetic  4.48 us (2%)
    pallas_call x1, Pallas kernels, output_call(): pl.pallas_call(output_kernel, out_shape=jax.ShapeDtypeStruct((256, dim),...  42.9 us
    pallas_call x1, Pallas kernels, att_call(): pl.pallas_call(att_kernel, grid_spec=grid_spec, out_shape=[jax.ShapeDtype...  35.5 us
    pallas_call x1, Pallas kernels, hidden_call(): pl.pallas_call(hidden_kernel, out_shape=[jax.ShapeDtypeStruct((128, dim),...  29.3 us
    pallas_call x1, Pallas kernels, combine_call(): pl.pallas_call(combine_kernel, out_shape=jax.ShapeDtypeStruct((16, 32, 12...  22.5 us
    pallas_call x1, Pallas kernels, qkv_call(): pl.pallas_call(functools.partial(qkv_kernel, nq=nq, nk=nk), grid=(nq + nk...  22.3 us
    pallas_call x1, Pallas kernels, gate_up_call(): pl.pallas_call(gate_up_kernel, grid_spec=pltpu.PrefetchScalarGridSpec(num...  15.3 us
    pallas_call x1, Pallas kernels, down_call(): pl.pallas_call(down_kernel, grid_spec=pltpu.PrefetchScalarGridSpec(num_sc...  12 us
    dot_general x1, matrix products, local_step(): part = jnp.dot(o, wo_loc, preferred_element_type=jnp.float32)  9.71 us

profile of v1, /device:TPU:0, one launch (start us, length us, event | category | flops | bytes accessed | tf_op | source)
XLA Modules:
  0.0 207.0 jit_solution(9547765217014075454)
XLA Ops:
  0.7 0.7 convert_element_type.9
  1.3 1.3 reshape.50.g_ref
  2.7 1.3 reshape.57.g_ref
  4.0 1.6 constant_dynamic-slice_fusion.x_ref
  5.6 0.5 fusion
  6.1 0.8 pad_maximum_fusion
  6.9 22.3 %qkv.1 = bf16[256,3072]{1,0:T(8,128)(2,1)} custom-call(bf16[256,5120]{1,0:T(8,128)(2,1)} %x_ref.1, bf16[1,5120]{1,0:T(2,128)(2,1)} %reshape.50.g_ref, f32[256,128]{1,0:T(8,128)} %get-tuple-element.22.cos_ref, f32[256,128]{1,0:T(8,128)} %get-tuple-element.23.sin_ref, bf16[5120,2048]{1,0:T(8,128)(2,1)} %wq_ref.1, bf16[5120,512]{1,0:T(8,128)(2,1)} %wk_ref.1, ...), custom_call_target="tpu_custom_call" | custom-call | tf_op jit(solution)/shard_map/qkv/pallas_call | solution.py:54
  29.2 1.1 fusion.1
  30.3 1.3 slice.12
  31.6 1.3 reshape.51.q_ref
  32.9 0.1 reshape.53
  33.0 0.1 reshape.52
  33.1 1.2 maximum_convert_fusion.kn_ref
  34.3 1.2 maximum_convert_fusion.1.vn_ref
  35.5 35.5 %att.1 = (bf16[256,128,128]{2,1,0:T(8,128)(2,1)}, bf16[256,128,128]{2,1,0:T(8,128)(2,1)}, f32[128,32,128]{2,1,0:T(8,128)}, f32[32,128]{1,0:T(8,128)}, f32[32,128]{1,0:T(8,128)}) custom-call(s32[256]{0:T(256)} %lens_ref.1, s32[1]{0:T(128)} %bitcast.1.base_ref, bf16[128,32,128]{2,1,0:T(8,128)(2,1)} %reshape.51.q_ref, ...), custom_call_target="tpu_custom_call" | custom-call | tf_op jit(solution)/shard_map/att/pallas_call | solution.py:147
  71.0 22.5 %combine.1 = bf16[16,32,128]{2,1,0:T(8,128)(2,1)} custom-call(f32[128,32,128]{2,1,0:T(8,128)} %get-tuple-element.10.mix_ref, f32[32,128]{1,0:T(8,128)} %get-tuple-element.11.m_ref, f32[32,128]{1,0:T(8,128)} %get-tuple-element.12.l_ref), custom_call_target="tpu_custom_call" | custom-call | tf_op jit(solution)/shard_map/combine/pallas_call | solution.py:252
  93.5 1.0 reshape.56
  94.4 9.7 %fusion.2.part_ref = f32[32,5120]{1,0:T(8,128)} fusion(bf16[32,2048]{1,0:T(8,128)(2,1)S(1)} %reshape.56, bf16[2048,5120]{1,0:T(8,128)(2,1)} %param.21), kind=kOutput, calls=%fused_computation.10 | convolution fusion | flops 671088640 | bytes 21757952 | tf_op jit(solution)/shard_map/dot_general | solution.py:506
  104.1 29.3 %hidden.1 = (bf16[128,5120]{1,0:T(8,128)(2,1)}, f32[16,5120]{1,0:T(8,128)}) custom-call(f32[32,5120]{1,0:T(8,128)} %fusion.2.part_ref, bf16[16,5120]{1,0:T(8,128)(2,1)} %constant_dynamic-slice_fusion.x_ref, bf16[1,5120]{1,0:T(2,128)(2,1)} %reshape.57.g_ref), custom_call_target="tpu_custom_call" | custom-call | tf_op jit(solution)/shard_map/hidden/pallas_call | solution.py:323
  133.4 15.3 %gate_up.1.m_ref = bf16[128,1792]{1,0:T(8,128)(2,1)} custom-call(s32[1]{0:T(128)} %bitcast.idx_ref, bf16[128,5120]{1,0:T(8,128)(2,1)} %get-tuple-element.13.h_ref, bf16[5120,7168]{1,0:T(8,128)(2,1)} %wg_ref.1, bf16[5120,7168]{1,0:T(8,128)(2,1)} %wu_ref.1), custom_call_target="tpu_custom_call" | custom-call | tf_op jit(solution)/shard_map/gate_up/pallas_call | solution.py:349
  148.7 12.0 %down.1.part_ref = f32[128,5120]{1,0:T(8,128)} custom-call(s32[1]{0:T(128)} %bitcast.idx_ref, bf16[128,1792]{1,0:T(8,128)(2,1)} %gate_up.1.m_ref, bf16[7168,5120]{1,0:T(8,128)(2,1)} %wd_ref.1), custom_call_target="tpu_custom_call" | custom-call | tf_op jit(solution)/shard_map/down/pallas_call | solution.py:370
  160.7 42.9 %output.1 = bf16[256,5120]{1,0:T(8,128)(2,1)} custom-call(f32[128,5120]{1,0:T(8,128)} %down.1.part_ref, f32[16,5120]{1,0:T(8,128)} %get-tuple-element.14.hid_ref), custom_call_target="tpu_custom_call" | custom-call | tf_op jit(solution)/shard_map/output/pallas_call | solution.py:463
  203.6 3.4 %copy.17 = bf16[256,5120]{1,0:T(8,128)(2,1)} copy(bf16[256,5120]{1,0:T(8,128)(2,1)} %output.1) | data formatting | bytes 5242880
  (1 shorter events, 0.0 us)

commit v2 on v1

--- a/solution.py
+++ b/solution.py
@@ -1,7 +1,6 @@
-import functools
-
 import jax
 import jax.numpy as jnp
+import numpy as np
 from jax import lax
 from jax.experimental import pallas as pl
 from jax.experimental.pallas import tpu as pltpu
@@ -13,150 +12,191 @@
 VMEM_LIMIT = 60 * 1024 * 1024
 
 
-def qkv_kernel(x_ref, g_ref, cos_ref, sin_ref, wq_ref, wk_ref, wv_ref, out_ref, u_ref, *, nq, nk):
-    i = pl.program_id(0)
-
-    @pl.when(i == 0)
-    def _():
-        xf = x_ref[...].astype(jnp.float32)
+WN = 256
+RB = 32
+RING = 4
+PAIRS = 8
+
+
+def attend_kernel(lens_s, lens_ref, freq_ref, g_ref, x_hbm, wq, wk, wv, kc, vc, ko, vo, mix_ref, m_ref, l_ref,
+                  xb, u, wbuf, q_s, kn_s, vn_s, cos_s, sin_s, kbuf, vbuf, sx, sw, sk, sv, tk, tv):
+    rows, dim = xb.shape
+    nq, nk, nv = wq.shape[1] // WN, wk.shape[1] // WN, wv.shape[1] // WN
+    blocks = kc.shape[0] // RB
+    base = lax.axis_index("sp") * (kc.shape[1] // 4)
+
+    cx = pltpu.make_async_copy(x_hbm, xb, sx)
+    cx.start()
+
+    def weight(w, i, n):
+        return pltpu.make_async_copy(w.at[:, pl.ds(pl.multiple_of(i * WN, WN), WN)], wbuf.at[n], sw.at[n])
+
+    for i in range(nq):
+        weight(wq, i, i).start()
+    for i in range(nk):
+        weight(wk, i, nq + i).start()
+    for i in range(nv):
+        weight(wv, i, nq + nk + i).start()
+
+    def load(n):
+        r, t = pl.ds(n * RB, RB), n % RING
+        return pltpu.make_async_copy(kc.at[r], kbuf.at[t], sk.at[t]), pltpu.make_async_copy(vc.at[r], vbuf.at[t], sv.at[t])
+
+    def store(n):
+        r, t = pl.ds(n * RB, RB), n % RING
+        return pltpu.make_async_copy(kbuf.at[t], ko.at[r], tk.at[t]), pltpu.make_async_copy(vbuf.at[t], vo.at[r], tv.at[t])
+
+    for n in range(RING):
+        for cp in load(n):
+            cp.start()
+
+    eye = lax.broadcasted_iota(jnp.int32, (rows, rows), 0) == lax.broadcasted_iota(jnp.int32, (rows, rows), 1)
+    lens_f = lens_ref[...].astype(jnp.float32).reshape(1, rows)
+    pos = jnp.sum(jnp.where(eye, lens_f, 0.0), axis=1, keepdims=True)
+    angles = pos * freq_ref[...]
+    half = lax.broadcasted_iota(jnp.int32, (rows, 128), 1) < 64
+    cos_s[...] = jnp.cos(angles)
+    sin_a = jnp.sin(angles)
+    sin_s[...] = jnp.where(half, -sin_a, sin_a)
+    m_ref[...] = jnp.zeros_like(m_ref)
+    l_ref[...] = jnp.zeros_like(l_ref)
+
+    cx.wait()
+    gain = g_ref[...].astype(jnp.float32).reshape(1, dim)
+
+    def norm(i, carry):
+        r = pl.ds(pl.multiple_of(i * 32, 32), 32)
+        xf = xb[r, :].astype(jnp.float32)
         inv = lax.rsqrt(jnp.mean(xf * xf, axis=-1, keepdims=True) + NORM_EPS)
-        u_ref[...] = (xf * inv * g_ref[...].astype(jnp.float32)).astype(jnp.bfloat16)
-
-    def project(w_ref, rope):
-        y = jnp.dot(u_ref[...], w_ref[...], preferred_element_type=jnp.float32)
-        y = y.astype(jnp.bfloat16)
-        if rope:
-            for h in range(y.shape[1] // 128):
-                t = y[:, h * 128 : (h + 1) * 128].astype(jnp.float32)
-                r = t * cos_ref[...] + pltpu.roll(t, 64, 1) * sin_ref[...]
-                out_ref[:, h * 128 : (h + 1) * 128] = r.astype(jnp.bfloat16)
-        else:
-            out_ref[...] = y
-
-    @pl.when(i < nq)
-    def _():
-        project(wq_ref, True)
-
-    @pl.when(jnp.logical_and(i >= nq, i < nq + nk))
-    def _():
-        project(wk_ref, True)
-
-    @pl.when(i >= nq + nk)
-    def _():
-        project(wv_ref, False)
-
-
-def qkv_call(x_tok, g_attn, cos_f, sin_f, wq, wk, wv):
-    rows, dim = x_tok.shape
-    bn = 256
-    nq, nk, nv = wq.shape[1] // bn, wk.shape[1] // bn, wv.shape[1] // bn
-    whole = lambda i: (0, 0)
-    return pl.pallas_call(
-        functools.partial(qkv_kernel, nq=nq, nk=nk),
-        grid=(nq + nk + nv,),
-        in_specs=[
-            pl.BlockSpec((rows, dim), whole),
-            pl.BlockSpec((1, dim), whole),
-            pl.BlockSpec((rows, 128), whole),
-            pl.BlockSpec((rows, 128), whole),
-            pl.BlockSpec((dim, bn), lambda i: (0, jnp.minimum(i, nq - 1))),
-            pl.BlockSpec((dim, bn), lambda i: (0, jnp.clip(i - nq, 0, nk - 1))),
-            pl.BlockSpec((dim, bn), lambda i: (0, jnp.clip(i - nq - nk, 0, nv - 1))),
-        ],
-        out_specs=pl.BlockSpec((rows, bn), lambda i: (0, i)),
-        out_shape=jax.ShapeDtypeStruct((rows, (nq + nk + nv) * bn), jnp.bfloat16),
-        scratch_shapes=[pltpu.VMEM((rows, dim), jnp.bfloat16)],
-        compiler_params=pltpu.CompilerParams(vmem_limit_bytes=VMEM_LIMIT),
-        name="qkv",
-    )(x_tok, g_attn.reshape(1, dim), cos_f, sin_f, wq, wk, wv)
-
-
-PAIRS = 8
-
-
-def att_kernel(lens_ref, base_ref, q_ref, kn_ref, vn_ref, k_ref, v_ref, ko_ref, vo_ref, mix_ref, m_ref, l_ref):
-    step = pl.program_id(0)
-    base = base_ref[0]
-
-    @pl.when(step == 0)
-    def _():
-        m_ref[...] = jnp.zeros_like(m_ref)
-        l_ref[...] = jnp.zeros_like(l_ref)
-
-    row = lax.broadcasted_iota(jnp.int32, (128, 128), 0)
-    row_pos = base + row // 4
+        u[r, :] = (xf * inv * gain).astype(jnp.bfloat16)
+        return carry
+
+    lax.fori_loop(0, rows // 32, norm, 0)
+
+    def rope(t):
+        return (t * cos_s[...] + pltpu.roll(t, 64, 1) * sin_s[...]).astype(jnp.bfloat16).astype(jnp.float32)
+
+    def project(w, i, n):
+        weight(w, i, n).wait()
+        y = jnp.dot(u[...], wbuf[n], preferred_element_type=jnp.float32)
+        return y.astype(jnp.bfloat16).astype(jnp.float32)
+
+    def q_chunk(i, carry):
+        y = project(wq, i, i)
+        for t in range(WN // 128):
+            q_s[pl.ds(i * (WN // 128) + t, rows, stride=16), :] = rope(y[:, t * 128 : (t + 1) * 128])
+        return carry
+
+    lax.fori_loop(0, nq, q_chunk, 0)
+    for w, count, first, dst, turn in ((wk, nk, nq, kn_s, True), (wv, nv, nq + nk, vn_s, False)):
+
+        def kv_chunk(i, carry, w=w, first=first, dst=dst, turn=turn):
+            y = project(w, i, first + i)
+            for t in range(WN // 128):
+                head = y[:, t * 128 : (t + 1) * 128]
+                head = rope(head) if turn else head
+                for again in (0, 4):
+                    dst[pl.ds(i * (WN // 128) + t + again, rows, stride=8), :] = head
+            return carry
+
+        lax.fori_loop(0, count, kv_chunk, 0)
+
+    row_pos = base + lax.broadcasted_iota(jnp.int32, (128, 128), 0) // 4
     ri = lax.broadcasted_iota(jnp.int32, (32, 256), 0)
     ci = lax.broadcasted_iota(jnp.int32, (32, 256), 1)
     same = jnp.logical_and(ri // 16 == ci // 128, (ri % 16) // 4 == ci % 4)
     col_pos = jnp.where(same, base + (ci % 128) // 4, 1 << 30)
-    first = ri < 16
+    upper = ri < 16
     lane = lax.broadcasted_iota(jnp.int32, (32, 128), 1)
     scale = 128.0 ** -0.5
-    m_all, l_all = m_ref[...], l_ref[...]
-    for j in range(PAIRS):
-        pair = step * PAIRS + j
-        p0 = lens_ref[2 * pair]
-        p1 = lens_ref[2 * pair + 1]
-        ks, vs = [], []
-        for t, p in ((0, p0), (1, p1)):
-            b = 2 * j + t
-            hit = row_pos == p
-            for src, new, dst, acc in ((k_ref, kn_ref, ko_ref, ks), (v_ref, vn_ref, vo_ref, vs)):
-                old = src[b].astype(jnp.float32)
-                add = jnp.broadcast_to(new[b][None], (16, 8, 128)).reshape(128, 128)
-                val = jnp.where(hit, add, old).astype(jnp.bfloat16)
-                dst[b] = val
-                acc.append(val)
-        kk = jnp.concatenate(ks, axis=0)
-        vv = jnp.concatenate(vs, axis=0)
-        s = lax.dot_general(q_ref[j], kk, (((1,), (1,)), ((), ())), preferred_element_type=jnp.float32) * scale
-        valid = col_pos <= jnp.where(first, p0, p1)
-        s = jnp.where(valid, s, -1e30)
-        m = jnp.max(s, axis=1, keepdims=True)
-        w = jnp.where(valid, jnp.exp(s - m), 0.0)
-        l = jnp.sum(w, axis=1, keepdims=True)
-        mix_ref[j] = jnp.dot(w.astype(jnp.bfloat16), vv, preferred_element_type=jnp.float32)
-        m_all = jnp.where(lane == pair, m, m_all)
-        l_all = jnp.where(lane == pair, l, l_all)
-    m_ref[...] = m_all
-    l_ref[...] = l_all
-
-
-def att_call(seq_lens, base, q, kn, vn, k2, v2):
+
+    for n in range(blocks):
+        slot = n % RING
+        for cp in load(n):
+            cp.wait()
+
+        def group(g, carry, n=n, slot=slot):
+            m_all, l_all = m_ref[...], l_ref[...]
+            for j in range(PAIRS):
+                local = g * PAIRS + j
+                pair = n * (RB // 2) + local
+                p0 = lens_s[2 * pair]
+                p1 = lens_s[2 * pair + 1]
+                ks, vs = [], []
+                for t, p in ((0, p0), (1, p1)):
+                    b = 2 * local + t
+                    new = pl.ds(pl.multiple_of(8 * (2 * pair + t), 8), 8)
+                    hit = row_pos == p
+                    for buf, fresh, acc in ((kbuf, kn_s, ks), (vbuf, vn_s, vs)):
+                        old = buf[slot, b].astype(jnp.float32)
+                        add = jnp.broadcast_to(fresh[new, :][None], (16, 8, 128)).reshape(128, 128)
+                        val = jnp.where(hit, add, old).astype(jnp.bfloat16)
+                        buf[slot, b] = val
+                        acc.append(val)
+                kk = jnp.concatenate(ks, axis=0)
+                vv = jnp.concatenate(vs, axis=0)
+                q = q_s[pl.ds(pl.multiple_of(32 * pair, 32), 32), :].astype(jnp.bfloat16)
+                s = lax.dot_general(q, kk, (((1,), (1,)), ((), ())), preferred_element_type=jnp.float32) * scale
+                valid = col_pos <= jnp.where(upper, p0, p1)
+                s = jnp.where(valid, s, -1e30)
+                m = jnp.max(s, axis=1, keepdims=True)
+                w = jnp.where(valid, jnp.exp(s - m), 0.0)
+                l = jnp.sum(w, axis=1, keepdims=True)
+                mix_ref[pair] = jnp.dot(w.astype(jnp.bfloat16), vv, preferred_element_type=jnp.float32)
+                m_all = jnp.where(lane == pair, m, m_all)
+                l_all = jnp.where(lane == pair, l, l_all)
+            m_ref[...] = m_all
+            l_ref[...] = l_all
+            return carry
+
+        lax.fori_loop(0, RB // 2 // PAIRS, group, 0)
+        for cp in store(n):
+            cp.start()
+        if n >= 1 and n - 1 + RING < blocks:
+            for cp in store(n - 1):
+                cp.wait()
+            for cp in load(n - 1 + RING):
+                cp.start()
+    for n in range(blocks - RING, blocks):
+        for cp in store(n):
+            cp.wait()
+
+
+def attend_call(seq_lens, freq, g_attn, x_tok, wq, wk, wv, k2, v2):
+    rows, dim = x_tok.shape
+    chunks = (wq.shape[1] + wk.shape[1] + wv.shape[1]) // WN
     batch = k2.shape[0]
-    nb = 2 * PAIRS
-    blk = lambda i, *_: (i, 0, 0)
-    grid_spec = pltpu.PrefetchScalarGridSpec(
-        num_scalar_prefetch=2,
-        grid=(batch // nb,),
-        in_specs=[
-            pl.BlockSpec((PAIRS, 32, 128), blk),
-            pl.BlockSpec((nb, 8, 128), blk),
-            pl.BlockSpec((nb, 8, 128), blk),
-            pl.BlockSpec((nb, 128, 128), blk),
-            pl.BlockSpec((nb, 128, 128), blk),
+    vm = pl.BlockSpec(memory_space=pltpu.VMEM)
+    hbm = pl.BlockSpec(memory_space=pl.ANY)
+    f32, bf16 = jnp.float32, jnp.bfloat16
+    dma = pltpu.SemaphoreType.DMA
+    return pl.pallas_call(
+        attend_kernel,
+        in_specs=[pl.BlockSpec(memory_space=pltpu.SMEM), vm, vm, vm] + [hbm] * 6,
+        out_specs=[hbm, hbm, vm, vm, vm],
+        out_shape=[
+            jax.ShapeDtypeStruct(k2.shape, bf16),
+            jax.ShapeDtypeStruct(v2.shape, bf16),
+            jax.ShapeDtypeStruct((batch // 2, 32, 128), f32),
+            jax.ShapeDtypeStruct((32, 128), f32),
+            jax.ShapeDtypeStruct((32, 128), f32),
         ],
-        out_specs=[
-            pl.BlockSpec((nb, 128, 128), blk),
-            pl.BlockSpec((nb, 128, 128), blk),
-            pl.BlockSpec((PAIRS, 32, 128), blk),
-            pl.BlockSpec((32, 128), lambda i, *_: (0, 0)),
-            pl.BlockSpec((32, 128), lambda i, *_: (0, 0)),
-        ],
-    )
-    return pl.pallas_call(
-        att_kernel,
-        grid_spec=grid_spec,
-        out_shape=[
-            jax.ShapeDtypeStruct(k2.shape, jnp.bfloat16),
-            jax.ShapeDtypeStruct(v2.shape, jnp.bfloat16),
-            jax.ShapeDtypeStruct((batch // 2, 32, 128), jnp.float32),
-            jax.ShapeDtypeStruct((32, 128), jnp.float32),
-            jax.ShapeDtypeStruct((32, 128), jnp.float32),
+        scratch_shapes=[
+            pltpu.VMEM((rows, dim), bf16),
+            pltpu.VMEM((rows, dim), bf16),
+            pltpu.VMEM((chunks, dim, WN), bf16),
+            pltpu.VMEM((batch * 16, 128), f32),
+            pltpu.VMEM((batch * 8, 128), f32),
+            pltpu.VMEM((batch * 8, 128), f32),
+            pltpu.VMEM((rows, 128), f32),
+            pltpu.VMEM((rows, 128), f32),
+            pltpu.VMEM((RING, RB, 128, 128), bf16),
+            pltpu.VMEM((RING, RB, 128, 128), bf16),
+            dma, dma((chunks,)), dma((RING,)), dma((RING,)), dma((RING,)), dma((RING,)),
         ],
         compiler_params=pltpu.CompilerParams(vmem_limit_bytes=VMEM_LIMIT),
-        name="att",
-    )(seq_lens, base, q, kn, vn, k2, v2)
+        name="attend",
+    )(seq_lens, seq_lens, freq, g_attn, x_tok, wq, wk, wv, k2, v2)
 
 
 def coords():
@@ -272,8 +312,11 @@
     )(mix, m, l)
 
 
-def hidden_kernel(part_ref, x_ref, g_ref, h_ref, hid_ref, zb, hbuf, sz, rz, ss, rs, sd, rd):
+def hidden_kernel(part_ref, x_hbm, g_ref, h_ref, hid_ref, x_ref, zb, hbuf, sx, sz, rz, ss, rs, sd, rd):
     z, y, x, c = coords()
+    at = pl.multiple_of(32 * (y * 4 + x * 2 + c) + 16 * z, 16)
+    cx = pltpu.make_async_copy(x_hbm.at[pl.ds(at, 16)], x_ref, sx)
+    cx.start()
     partner = device(z, y, x, 1 - c)
     zdev = device(1 - z, y, x, c)
     z1, x1 = z + c * (1 - 2 * z), x + (1 - c) * (1 - 2 * x)
@@ -282,6 +325,7 @@
     greet([partner, dev1, dev2])
     cz = remote(part_ref.at[pl.ds(16 * (1 - z), 16)], zb, sz, rz, zdev)
     cz.start()
+    cx.wait()
     cz.wait_recv()
     own = part_ref[pl.ds(pl.multiple_of(16 * z, 16), 16), :]
     hid = (x_ref[...].astype(jnp.float32) + (own + zb[...])).astype(jnp.bfloat16).astype(jnp.float32)
@@ -289,7 +333,7 @@
     inv = lax.rsqrt(jnp.mean(hid * hid, axis=-1, keepdims=True) + NORM_EPS)
     slot = lambda zz, xx, cc: (xx * 2 + cc) * 2 + zz
     mine = slot(z, x, c)
-    hbuf[mine] = (hid * inv * g_ref[...].astype(jnp.float32)).astype(jnp.bfloat16).astype(jnp.float32)
+    hbuf[mine] = (hid * inv * g_ref[...].astype(jnp.float32).reshape(1, hid.shape[1])).astype(jnp.bfloat16).astype(jnp.float32)
 
     def send(sl, dev, s, r, n):
         cp = remote(hbuf.at[sl], hbuf.at[sl], s.at[n], r.at[n], dev)
@@ -315,7 +359,7 @@
         cp.wait_send()
 
 
-def hidden_call(part, xs, g):
+def hidden_call(part, x_tok, g):
     vm = pl.BlockSpec(memory_space=pltpu.VMEM)
     f32 = jnp.float32
     dim = part.shape[1]
@@ -323,16 +367,17 @@
     return pl.pallas_call(
         hidden_kernel,
         out_shape=[jax.ShapeDtypeStruct((128, dim), jnp.bfloat16), jax.ShapeDtypeStruct((16, dim), f32)],
-        in_specs=[vm, vm, vm],
+        in_specs=[vm, pl.BlockSpec(memory_space=pl.ANY), vm],
         out_specs=[vm, vm],
         scratch_shapes=[
+            pltpu.VMEM((16, dim), jnp.bfloat16),
             pltpu.VMEM((16, dim), f32),
             pltpu.VMEM((8, 16, dim), f32),
-            dma, dma, dma((3,)), dma((3,)), dma((4,)), dma((4,)),
+            dma, dma, dma, dma((3,)), dma((3,)), dma((4,)), dma((4,)),
         ],
         compiler_params=pltpu.CompilerParams(collective_id=1, has_side_effects=True, vmem_limit_bytes=VMEM_LIMIT),
         name="hidden",
-    )(part, xs, g.reshape(1, dim))
+    )(part, x_tok, g)
 
 
 def gate_up_kernel(idx_ref, h_ref, wg_ref, wu_ref, m_ref):
@@ -486,26 +531,14 @@
     def local_step(x_tok, seq_lens, k_blk, v_blk, g_attn, wq_loc, wk_loc, wv_loc, wo_loc, g_mlp, wg_loc, wu_loc, wd_loc):
         batch, seq_blk, kv_loc, head_dim = k_blk.shape
         q_loc = wq_loc.shape[1] // head_dim
-        half = head_dim // 2
-        z, sp = lax.axis_index("tp"), lax.axis_index("sp")
-        inv_freq = jnp.power(jnp.float32(ROPE_BASE), jnp.arange(half, dtype=jnp.float32) * (-2.0 / head_dim))
-        angles = seq_lens.astype(jnp.float32)[:, None] * inv_freq
-        cos_a, sin_a = jnp.cos(angles), jnp.sin(angles)
-        cos_f = jnp.concatenate([cos_a, cos_a], axis=-1)
-        sin_f = jnp.concatenate([-sin_a, sin_a], axis=-1)
-        qkv = qkv_call(x_tok, g_attn, cos_f, sin_f, wq_loc, wk_loc, wv_loc)
-        qw, kw = q_loc * head_dim, kv_loc * head_dim
-        q = qkv[:, :qw].reshape(batch // 2, 2 * q_loc, head_dim)
-        twice = lambda t: jnp.concatenate([t, t], axis=1).astype(jnp.float32)
-        kn = twice(qkv[:, qw : qw + kw].reshape(batch, kv_loc, head_dim))
-        vn = twice(qkv[:, qw + kw :].reshape(batch, kv_loc, head_dim))
-        base = (sp * seq_blk).astype(jnp.int32).reshape(1)
+        sp = lax.axis_index("sp")
+        freq = ROPE_BASE ** (np.arange(head_dim // 2, dtype=np.float64) * (-2.0 / head_dim))
+        freq = jnp.asarray(np.concatenate([freq, freq])[None].astype(np.float32))
         flat = (batch, seq_blk * kv_loc, head_dim)
-        k_out, v_out, mix, m, l = att_call(seq_lens, base, q, kn, vn, k_blk.reshape(flat), v_blk.reshape(flat))
+        k_out, v_out, mix, m, l = attend_call(seq_lens, freq, g_attn, x_tok, wq_loc, wk_loc, wv_loc, k_blk.reshape(flat), v_blk.reshape(flat))
         o = combine_call(mix, m, l).reshape(32, q_loc * head_dim)
         part = jnp.dot(o, wo_loc, preferred_element_type=jnp.float32)
-        xs = lax.dynamic_slice_in_dim(x_tok, 32 * sp + 16 * z, 16, 0)
-        h, hid = hidden_call(part, xs, g_mlp)
+        h, hid = hidden_call(part, x_tok, g_mlp)
         idx = (sp % 4).astype(jnp.int32).reshape(1)
         act = gate_up_call(idx, h, wg_loc, wu_loc, 4)
         down = down_call(idx, act, wd_loc)

time: 208 us -> 197 us (0.947)
  local copies, waits for them, and re-layouts: 12.4 us -> 4.37 us
  other arithmetic: 4.48 us -> 0 us
    reshape x5 -> x0, local copies, waits for them, and re-layouts: 4.08 us -> none  [the longest x1 1.32 us: qkv_call(): g_attn.reshape(1, dim)]
    convert_element_type x3 -> x0, other arithmetic: 3.1 us -> none  [the longest x2 2.42 us: local_step(): twice = lambda t: jnp.concatenate([t, t], axis=1).astype(jnp.float32)]
    pallas_call x2 -> x1, Pallas kernels: 57.8 us -> 60.4 us  [attend_call(): pl.pallas_call(attend_kernel, in_specs=[pl.BlockSpec(memory_space=pltpu.S...]
    slice x2 -> x0, local copies, waits for them, and re-layouts: 2.36 us -> none  [the longest x1 1.3 us: local_step(): q = qkv[:, :qw].reshape(batch // 2, 2 * q_loc, head_dim)]
where the time goes in v2:
time: 197 us
  Pallas kernels  182 us (92%)
  matrix products  9.72 us (5%)
  local copies, waits for them, and re-layouts  4.37 us (2%)
    pallas_call x1, Pallas kernels, attend_call(): pl.pallas_call(attend_kernel, in_specs=[pl.BlockSpec(memory_space=pltpu.S...  60.4 us
    pallas_call x1, Pallas kernels, output_call(): pl.pallas_call(output_kernel, out_shape=jax.ShapeDtypeStruct((256, dim),...  42.9 us
    pallas_call x1, Pallas kernels, hidden_call(): pl.pallas_call(hidden_kernel, out_shape=[jax.ShapeDtypeStruct((128, dim),...  29.2 us
    pallas_call x1, Pallas kernels, combine_call(): pl.pallas_call(combine_kernel, out_shape=jax.ShapeDtypeStruct((16, 32, 12...  22.5 us
    pallas_call x1, Pallas kernels, gate_up_call(): pl.pallas_call(gate_up_kernel, grid_spec=pltpu.PrefetchScalarGridSpec(num...  15.3 us
    pallas_call x1, Pallas kernels, down_call(): pl.pallas_call(down_kernel, grid_spec=pltpu.PrefetchScalarGridSpec(num_sc...  12 us
    dot_general x1, matrix products, local_step(): part = jnp.dot(o, wo_loc, preferred_element_type=jnp.float32)  9.72 us

profile of v2, /device:TPU:0, one launch (start us, length us, event | category | flops | bytes accessed | tf_op | source)
XLA Modules:
  0.0 197.0 jit_solution(2171576503618990953)
XLA Ops:
  0.6 60.4 %attend.1 = (bf16[256,128,128]{2,1,0:T(8,128)(2,1)}, bf16[256,128,128]{2,1,0:T(8,128)(2,1)}, f32[128,32,128]{2,1,0:T(8,128)}, f32[32,128]{1,0:T(8,128)}, f32[32,128]{1,0:T(8,128)}) custom-call(s32[256]{0:T(256)} %lens_ref.1, s32[256]{0:T(256)} %lens_ref.1, f32[1,128]{1,0:T(1,128)} %constant.19.clone.freq_ref, bf16[5120]{0:T(1024)(128)(2,1)} %g_ref.2, ...), custom_call_target="tpu_custom_call" | custom-call | tf_op jit(solution)/shard_map/attend/pallas_call | solution.py:173
  61.1 22.5 %combine.1 = bf16[16,32,128]{2,1,0:T(8,128)(2,1)} custom-call(f32[128,32,128]{2,1,0:T(8,128)} %get-tuple-element.10.mix_ref, f32[32,128]{1,0:T(8,128)} %get-tuple-element.11.m_ref, f32[32,128]{1,0:T(8,128)} %get-tuple-element.12.l_ref), custom_call_target="tpu_custom_call" | custom-call | tf_op jit(solution)/shard_map/combine/pallas_call | solution.py:292
  83.6 1.0 reshape.27
  84.5 9.7 %fusion.part_ref = f32[32,5120]{1,0:T(8,128)} fusion(bf16[32,2048]{1,0:T(8,128)(2,1)S(1)} %reshape.27, bf16[2048,5120]{1,0:T(8,128)(2,1)} %param.22), kind=kOutput, calls=%fused_computation | convolution fusion | flops 671088640 | bytes 21757952 | tf_op jit(solution)/shard_map/dot_general | solution.py:540
  94.3 29.2 %hidden.1 = (bf16[128,5120]{1,0:T(8,128)(2,1)}, f32[16,5120]{1,0:T(8,128)}) custom-call(f32[32,5120]{1,0:T(8,128)} %fusion.part_ref, bf16[256,5120]{1,0:T(8,128)(2,1)} %x_hbm.3, bf16[5120]{0:T(1024)(128)(2,1)} %g_ref.3), custom_call_target="tpu_custom_call" | custom-call | tf_op jit(solution)/shard_map/hidden/pallas_call | solution.py:367
  123.4 15.3 %gate_up.1.m_ref = bf16[128,1792]{1,0:T(8,128)(2,1)} custom-call(s32[1]{0:T(128)} %bitcast.idx_ref, bf16[128,5120]{1,0:T(8,128)(2,1)} %get-tuple-element.13.h_ref, bf16[5120,7168]{1,0:T(8,128)(2,1)} %wg_ref.1, bf16[5120,7168]{1,0:T(8,128)(2,1)} %wu_ref.1), custom_call_target="tpu_custom_call" | custom-call | tf_op jit(solution)/shard_map/gate_up/pallas_call | solution.py:394
  138.7 12.0 %down.1.part_ref = f32[128,5120]{1,0:T(8,128)} custom-call(s32[1]{0:T(128)} %bitcast.idx_ref, bf16[128,1792]{1,0:T(8,128)(2,1)} %gate_up.1.m_ref, bf16[7168,5120]{1,0:T(8,128)(2,1)} %wd_ref.1), custom_call_target="tpu_custom_call" | custom-call | tf_op jit(solution)/shard_map/down/pallas_call | solution.py:415
  150.7 42.9 %output.1 = bf16[256,5120]{1,0:T(8,128)(2,1)} custom-call(f32[128,5120]{1,0:T(8,128)} %down.1.part_ref, f32[16,5120]{1,0:T(8,128)} %get-tuple-element.14.hid_ref), custom_call_target="tpu_custom_call" | custom-call | tf_op jit(solution)/shard_map/output/pallas_call | solution.py:508
  193.6 3.4 %copy.18 = bf16[256,5120]{1,0:T(8,128)(2,1)} copy(bf16[256,5120]{1,0:T(8,128)(2,1)} %output.1) | data formatting | bytes 5242880

commit v3 on v2

--- a/solution.py
+++ b/solution.py
@@ -10,12 +10,14 @@
 NORM_EPS = 1e-5
 MESH = pl.DeviceIdType.MESH
 VMEM_LIMIT = 60 * 1024 * 1024
-
-
-WN = 256
+VMEM_MOST = 67043328
+
+
+WN = 512
 RB = 32
 RING = 4
-PAIRS = 8
+AHEAD = 2
+PAIRS = 16
 
 
 def attend_kernel(lens_s, lens_ref, freq_ref, g_ref, x_hbm, wq, wk, wv, kc, vc, ko, vo, mix_ref, m_ref, l_ref,
@@ -31,12 +33,9 @@
     def weight(w, i, n):
         return pltpu.make_async_copy(w.at[:, pl.ds(pl.multiple_of(i * WN, WN), WN)], wbuf.at[n], sw.at[n])
 
-    for i in range(nq):
-        weight(wq, i, i).start()
-    for i in range(nk):
-        weight(wk, i, nq + i).start()
-    for i in range(nv):
-        weight(wv, i, nq + nk + i).start()
+    chunks = [(wq, i) for i in range(nq)] + [(wk, i) for i in range(nk)] + [(wv, i) for i in range(nv)]
+    for n in range(AHEAD):
+        weight(*chunks[n], n).start()
 
     def load(n):
         r, t = pl.ds(n * RB, RB), n % RING
@@ -45,10 +44,6 @@
     def store(n):
         r, t = pl.ds(n * RB, RB), n % RING
         return pltpu.make_async_copy(kbuf.at[t], ko.at[r], tk.at[t]), pltpu.make_async_copy(vbuf.at[t], vo.at[r], tv.at[t])
-
-    for n in range(RING):
-        for cp in load(n):
-            cp.start()
 
     eye = lax.broadcasted_iota(jnp.int32, (rows, rows), 0) == lax.broadcasted_iota(jnp.int32, (rows, rows), 1)
     lens_f = lens_ref[...].astype(jnp.float32).reshape(1, rows)
@@ -76,30 +71,24 @@
     def rope(t):
         return (t * cos_s[...] + pltpu.roll(t, 64, 1) * sin_s[...]).astype(jnp.bfloat16).astype(jnp.float32)
 
-    def project(w, i, n):
+    early = [lambda n=n: weight(*chunks[n], n).start() for n in range(AHEAD, len(chunks))]
+    early += [lambda n=n: [cp.start() for cp in load(n)] for n in range(min(RING, blocks))]
+    per = WN // 128
+    for n, (w, i) in enumerate(chunks):
         weight(w, i, n).wait()
-        y = jnp.dot(u[...], wbuf[n], preferred_element_type=jnp.float32)
-        return y.astype(jnp.bfloat16).astype(jnp.float32)
-
-    def q_chunk(i, carry):
-        y = project(wq, i, i)
-        for t in range(WN // 128):
-            q_s[pl.ds(i * (WN // 128) + t, rows, stride=16), :] = rope(y[:, t * 128 : (t + 1) * 128])
-        return carry
-
-    lax.fori_loop(0, nq, q_chunk, 0)
-    for w, count, first, dst, turn in ((wk, nk, nq, kn_s, True), (wv, nv, nq + nk, vn_s, False)):
-
-        def kv_chunk(i, carry, w=w, first=first, dst=dst, turn=turn):
-            y = project(w, i, first + i)
-            for t in range(WN // 128):
-                head = y[:, t * 128 : (t + 1) * 128]
-                head = rope(head) if turn else head
+        early.pop(0)()
+        y = jnp.dot(u[...], wbuf[n], preferred_element_type=jnp.float32).astype(jnp.bfloat16).astype(jnp.float32)
+        for t in range(per):
+            head = y[:, t * 128 : (t + 1) * 128]
+            head = head if w is wv else rope(head)
+            if w is wq:
+                q_s[pl.ds(i * per + t, rows, stride=16), :] = head
+            else:
+                dst = kn_s if w is wk else vn_s
                 for again in (0, 4):
-                    dst[pl.ds(i * (WN // 128) + t + again, rows, stride=8), :] = head
-            return carry
-
-        lax.fori_loop(0, count, kv_chunk, 0)
+                    dst[pl.ds(i * per + t + again, rows, stride=8), :] = head
+    for go in early:
+        go()
 
     row_pos = base + lax.broadcasted_iota(jnp.int32, (128, 128), 0) // 4
     ri = lax.broadcasted_iota(jnp.int32, (32, 256), 0)
@@ -142,7 +131,8 @@
                 m = jnp.max(s, axis=1, keepdims=True)
                 w = jnp.where(valid, jnp.exp(s - m), 0.0)
                 l = jnp.sum(w, axis=1, keepdims=True)
-                mix_ref[pair] = jnp.dot(w.astype(jnp.bfloat16), vv, preferred_element_type=jnp.float32)
+                mix_ref[pair, :16] = jnp.dot(w[:16, :128].astype(jnp.bfloat16), vs[0], preferred_element_type=jnp.float32)
+                mix_ref[pair, 16:] = jnp.dot(w[16:, 128:].astype(jnp.bfloat16), vs[1], preferred_element_type=jnp.float32)
                 m_all = jnp.where(lane == pair, m, m_all)
                 l_all = jnp.where(lane == pair, l, l_all)
             m_ref[...] = m_all
@@ -224,10 +214,13 @@
     return pltpu.make_async_remote_copy(src_ref=src, dst_ref=dst, send_sem=send, recv_sem=recv, device_id=dev, device_id_type=MESH)
 
 
-def combine_kernel(mix_ref, m_ref, l_ref, o_ref, got1, st_own, st1, comb, stc, got2, st2, s1, r1, s2, r2):
+def combine_kernel(mix_ref, m_ref, l_ref, wo, part_ref, o_s, wbuf, sw, got1, st_own, st1, comb, stc, got2, st2, s1, r1, s2, r2):
     z, y, x, c = coords()
     partner = device(z, y, x, 1 - c)
     chips = [(y, x), (y, 1 - x), (1 - y, x), (1 - y, 1 - x)]
+    weights = [pltpu.make_async_copy(wo.at[pl.ds(n * WN, WN)], wbuf.at[pl.ds(n * WN, WN)], sw.at[n]) for n in range(wo.shape[0] // WN)]
+    for cp in weights:
+        cp.start()
     greet([partner] + [device(z, b, a, c) for b, a in chips[1:]])
 
     st_own[0] = m_ref[...]
@@ -281,20 +274,30 @@
         acc = comb[0, j] * fs[0][:, j : j + 1]
         for k in (1, 2, 3):
             acc = acc + got2[k - 1, j] * fs[k][:, j : j + 1]
-        o_ref[j] = (acc / total[:, j : j + 1]).astype(jnp.bfloat16)
+        o_s[32 * j : 32 * j + 32, :] = acc / total[:, j : j + 1]
+    o = jnp.concatenate([o_s[pl.ds(h, 32, stride=16), :].astype(jnp.bfloat16) for h in range(16)], axis=1)
+    for cp in weights:
+        cp.wait()
+    for n in range(wo.shape[1] // WN):
+        cols = slice(n * WN, (n + 1) * WN)
+        part_ref[:, cols] = jnp.dot(o, wbuf[:, cols], preferred_element_type=jnp.float32)
     for cp in first + [stat1] + [stats2[k] for k in stats2] + [second[k] for k in second]:
         cp.wait_send()
 
 
-def combine_call(mix, m, l):
+def combine_call(mix, m, l, wo):
     vm = pl.BlockSpec(memory_space=pltpu.VMEM)
     f32 = jnp.float32
+    depth, dim = wo.shape
     return pl.pallas_call(
         combine_kernel,
-        out_shape=jax.ShapeDtypeStruct((16, 32, 128), jnp.bfloat16),
-        in_specs=[vm, vm, vm],
+        out_shape=jax.ShapeDtypeStruct((32, dim), f32),
+        in_specs=[vm, vm, vm, pl.BlockSpec(memory_space=pl.ANY)],
         out_specs=vm,
         scratch_shapes=[
+            pltpu.VMEM((512, 128), f32),
+            pltpu.VMEM((depth, dim), jnp.bfloat16),
+            pltpu.SemaphoreType.DMA((depth // WN,)),
             pltpu.VMEM((4, 16, 32, 128), f32),
             pltpu.VMEM((2, 32, 128), f32),
             pltpu.VMEM((2, 32, 128), f32),
@@ -309,14 +312,36 @@
         ],
         compiler_params=pltpu.CompilerParams(collective_id=0, has_side_effects=True, vmem_limit_bytes=VMEM_LIMIT),
         name="combine",
-    )(mix, m, l)
-
-
-def hidden_kernel(part_ref, x_hbm, g_ref, h_ref, hid_ref, x_ref, zb, hbuf, sx, sz, rz, ss, rs, sd, rd):
+    )(mix, m, l, wo)
+
+
+GN = 256
+KN = 1024
+HELD = 4096
+
+
+def hidden_kernel(part_ref, x_hbm, g_ref, wg, wu, wd, down_ref, hid_ref, x_ref, zb, hbuf, h_s, act, gbuf, ubuf, dbuf,
+                  sg, su, sdw, sx, sz, rz, ss, rs, sd, rd):
     z, y, x, c = coords()
+    depth = act.shape[1]
+    mine_from = (2 * x + c) * depth
+    gates, downs = depth // GN, wd.shape[1] // WN
+
+    def gate_load(w, buf, sem, n):
+        r = pl.ds(n * KN, KN)
+        return pltpu.make_async_copy(w.at[r, pl.ds(pl.multiple_of(mine_from, GN), depth)], buf.at[r], sem.at[n])
+
+    def down_load(n):
+        src = wd.at[pl.ds(pl.multiple_of(mine_from + n * GN, GN), GN), pl.ds(0, dbuf.shape[1])]
+        return pltpu.make_async_copy(src, dbuf.at[pl.ds(n * GN, GN)], sdw.at[n])
+
     at = pl.multiple_of(32 * (y * 4 + x * 2 + c) + 16 * z, 16)
     cx = pltpu.make_async_copy(x_hbm.at[pl.ds(at, 16)], x_ref, sx)
     cx.start()
+    loads = [gate_load(w, buf, sem, n) for n in range(wg.shape[0] // KN) for w, buf, sem in ((wg, gbuf, sg), (wu, ubuf, su))]
+    loads += [down_load(n) for n in range(gates)]
+    for cp in loads:
+        cp.start()
     partner = device(z, y, x, 1 - c)
     zdev = device(1 - z, y, x, c)
     z1, x1 = z + c * (1 - 2 * z), x + (1 - c) * (1 - 2 * x)
@@ -354,76 +379,59 @@
     for cp in (d0, d1, d2, d3):
         cp.wait_recv()
     for k in range(8):
-        h_ref[pl.ds(16 * k, 16), :] = hbuf[k].astype(jnp.bfloat16)
+        h_s[pl.ds(16 * k, 16), :] = hbuf[k].astype(jnp.bfloat16)
     for cp in (cz, a1, a2, a3, d0, d1, d2, d3):
         cp.wait_send()
-
-
-def hidden_call(part, x_tok, g):
+    up16 = lambda t: t.astype(jnp.bfloat16).astype(jnp.float32)
+    for cp in loads[: len(loads) - gates]:
+        cp.wait()
+    for n in range(gates):
+        cols = slice(n * GN, (n + 1) * GN)
+        gate = up16(jnp.dot(h_s[...], gbuf[:, cols], preferred_element_type=jnp.float32))
+        up = up16(jnp.dot(h_s[...], ubuf[:, cols], preferred_element_type=jnp.float32))
+        act[:, cols] = (jax.nn.silu(gate) * up).astype(jnp.bfloat16)
+    held = dbuf.shape[1]
+    rest = wd.shape[1] - held
+    spare = gbuf.at[pl.ds(0, depth), pl.ds(0, rest)]
+    last = pltpu.make_async_copy(wd.at[pl.ds(pl.multiple_of(mine_from, GN), depth), pl.ds(held, rest)], spare, sdw.at[gates])
+    last.start()
+    for cp in loads[len(loads) - gates :]:
+        cp.wait()
+    for n in range(downs):
+        if n * WN == held:
+            last.wait()
+        wide = dbuf[:, n * WN : (n + 1) * WN] if n * WN < held else gbuf[:depth, n * WN - held : (n + 1) * WN - held]
+        down_ref[:, n * WN : (n + 1) * WN] = jnp.dot(act[...], wide, preferred_element_type=jnp.float32)
+
+
+def hidden_call(part, x_tok, g, wg, wu, wd, ways):
     vm = pl.BlockSpec(memory_space=pltpu.VMEM)
     f32 = jnp.float32
     dim = part.shape[1]
     dma = pltpu.SemaphoreType.DMA
+    hbm = pl.BlockSpec(memory_space=pl.ANY)
+    depth = wg.shape[1] // ways
+    bf16 = jnp.bfloat16
     return pl.pallas_call(
         hidden_kernel,
-        out_shape=[jax.ShapeDtypeStruct((128, dim), jnp.bfloat16), jax.ShapeDtypeStruct((16, dim), f32)],
-        in_specs=[vm, pl.BlockSpec(memory_space=pl.ANY), vm],
+        out_shape=[jax.ShapeDtypeStruct((128, dim), f32), jax.ShapeDtypeStruct((16, dim), f32)],
+        in_specs=[vm, hbm, vm, hbm, hbm, hbm],
         out_specs=[vm, vm],
         scratch_shapes=[
-            pltpu.VMEM((16, dim), jnp.bfloat16),
+            pltpu.VMEM((16, dim), bf16),
             pltpu.VMEM((16, dim), f32),
             pltpu.VMEM((8, 16, dim), f32),
+            pltpu.VMEM((128, dim), bf16),
+            pltpu.VMEM((128, depth), bf16),
+            pltpu.VMEM((dim, depth), bf16),
+            pltpu.VMEM((dim, depth), bf16),
+            pltpu.VMEM((depth, HELD), bf16),
+            dma((dim // KN,)), dma((dim // KN,)), dma((depth // GN + 1,)),
             dma, dma, dma, dma((3,)), dma((3,)), dma((4,)), dma((4,)),
         ],
-        compiler_params=pltpu.CompilerParams(collective_id=1, has_side_effects=True, vmem_limit_bytes=VMEM_LIMIT),
+        compiler_params=pltpu.CompilerParams(collective_id=1, has_side_effects=True, vmem_limit_bytes=VMEM_MOST),
         name="hidden",
-    )(part, x_tok, g)
-
-
-def gate_up_kernel(idx_ref, h_ref, wg_ref, wu_ref, m_ref):
-    g = jnp.dot(h_ref[...], wg_ref[...], preferred_element_type=jnp.float32).astype(jnp.bfloat16).astype(jnp.float32)
-    u = jnp.dot(h_ref[...], wu_ref[...], preferred_element_type=jnp.float32).astype(jnp.bfloat16).astype(jnp.float32)
-    m_ref[...] = (jax.nn.silu(g) * u).astype(jnp.bfloat16)
-
-
-def gate_up_call(idx, h, wg, wu, ways):
-    rows, dim = h.shape
-    bn = 256
-    steps = wg.shape[1] // ways // bn
-    wspec = pl.BlockSpec((dim, bn), lambda i, s: (0, s[0] * steps + i))
-    return pl.pallas_call(
-        gate_up_kernel,
-        grid_spec=pltpu.PrefetchScalarGridSpec(
-            num_scalar_prefetch=1,
-            grid=(steps,),
-            in_specs=[pl.BlockSpec((rows, dim), lambda i, s: (0, 0)), wspec, wspec],
-            out_specs=pl.BlockSpec((rows, bn), lambda i, s: (0, i)),
-        ),
-        out_shape=jax.ShapeDtypeStruct((rows, steps * bn), jnp.bfloat16),
-        compiler_params=pltpu.CompilerParams(vmem_limit_bytes=VMEM_LIMIT),
-        name="gate_up",
-    )(idx, h, wg, wu)
-
-
-def down_kernel(idx_ref, m_ref, wd_ref, o_ref):
-    o_ref[...] = jnp.dot(m_ref[...], wd_ref[...], preferred_element_type=jnp.float32)
-
-
-def down_call(idx, m, wd):
-    rows, depth = m.shape
-    bn = 512
-    return pl.pallas_call(
-        down_kernel,
-        grid_spec=pltpu.PrefetchScalarGridSpec(
-            num_scalar_prefetch=1,
-            grid=(wd.shape[1] // bn,),
-            in_specs=[pl.BlockSpec((rows, depth), lambda i, s: (0, 0)), pl.BlockSpec((depth, bn), lambda i, s: (s[0], i))],
-            out_specs=pl.BlockSpec((rows, bn), lambda i, s: (0, i)),
-        ),
-        out_shape=jax.ShapeDtypeStruct((rows, wd.shape[1]), jnp.float32),
-        compiler_params=pltpu.CompilerParams(vmem_limit_bytes=VMEM_LIMIT),
-        name="down",
-    )(idx, m, wd)
+    )(part, x_tok, g, wg, wu, wd)
 
 
 COLORS = ((0, 1664), (1664, 1664), (3328, 1792))
@@ -531,17 +539,12 @@
     def local_step(x_tok, seq_lens, k_blk, v_blk, g_attn, wq_loc, wk_loc, wv_loc, wo_loc, g_mlp, wg_loc, wu_loc, wd_loc):
         batch, seq_blk, kv_loc, head_dim = k_blk.shape
         q_loc = wq_loc.shape[1] // head_dim
-        sp = lax.axis_index("sp")
         freq = ROPE_BASE ** (np.arange(head_dim // 2, dtype=np.float64) * (-2.0 / head_dim))
         freq = jnp.asarray(np.concatenate([freq, freq])[None].astype(np.float32))
         flat = (batch, seq_blk * kv_loc, head_dim)
         k_out, v_out, mix, m, l = attend_call(seq_lens, freq, g_attn, x_tok, wq_loc, wk_loc, wv_loc, k_blk.reshape(flat), v_blk.reshape(flat))
-        o = combine_call(mix, m, l).reshape(32, q_loc * head_dim)
-        part = jnp.dot(o, wo_loc, preferred_element_type=jnp.float32)
-        h, hid = hidden_call(part, x_tok, g_mlp)
-        idx = (sp % 4).astype(jnp.int32).reshape(1)
-        act = gate_up_call(idx, h, wg_loc, wu_loc, 4)
-        down = down_call(idx, act, wd_loc)
+        part = combine_call(mix, m, l, wo_loc)
+        down, hid = hidden_call(part, x_tok, g_mlp, wg_loc, wu_loc, wd_loc, 4)
         y_out = output_call(down, hid)
         return y_out, k_out.reshape(k_blk.shape), v_out.reshape(v_blk.shape)
 

time: 197 us -> 143 us (0.73)
  Pallas kernels: 182 us -> 139 us
  matrix products: 9.72 us -> 0 us
    pallas_call x1, Pallas kernels: 60.4 us -> 28.1 us  [attend_call(): pl.pallas_call(attend_kernel, in_specs=[pl.BlockSpec(memory_space=pltpu.S...]
    pallas_call x3 -> x1, Pallas kernels: 49.7 us -> 26.4 us  [combine_call(): pl.pallas_call(combine_kernel, out_shape=jax.ShapeDtypeStruct((32, dim),...]
    pallas_call x1, Pallas kernels: 29.2 us -> 40.7 us  [hidden_call(): pl.pallas_call(hidden_kernel, out_shape=[jax.ShapeDtypeStruct((128, dim),...]
    dot_general x1 -> x0, matrix products: 9.72 us -> none  [local_step(): part = jnp.dot(o, wo_loc, preferred_element_type=jnp.float32)]
where the time goes in v3:
time: 143 us
  Pallas kernels  139 us (97%)
  local copies, waits for them, and re-layouts  3.4 us (2%)
    pallas_call x1, Pallas kernels, output_call(): pl.pallas_call(output_kernel, out_shape=jax.ShapeDtypeStruct((256, dim),...  43.8 us
    pallas_call x1, Pallas kernels, hidden_call(): pl.pallas_call(hidden_kernel, out_shape=[jax.ShapeDtypeStruct((128, dim),...  40.7 us
    pallas_call x1, Pallas kernels, attend_call(): pl.pallas_call(attend_kernel, in_specs=[pl.BlockSpec(memory_space=pltpu.S...  28.1 us
    pallas_call x1, Pallas kernels, combine_call(): pl.pallas_call(combine_kernel, out_shape=jax.ShapeDtypeStruct((32, dim),...  26.4 us
    unnamed x1, local copies, waits for them, and re-layouts  3.4 us

profile of v3, /device:TPU:0, one launch (start us, length us, event | category | flops | bytes accessed | tf_op | source)
XLA Modules:
  0.0 143.1 jit_solution(17410829761937101531)
XLA Ops:
  0.6 28.1 %attend.1 = (bf16[256,128,128]{2,1,0:T(8,128)(2,1)}, bf16[256,128,128]{2,1,0:T(8,128)(2,1)}, f32[128,32,128]{2,1,0:T(8,128)}, f32[32,128]{1,0:T(8,128)}, f32[32,128]{1,0:T(8,128)}) custom-call(s32[256]{0:T(256)} %lens_ref.1, s32[256]{0:T(256)} %lens_ref.1, f32[1,128]{1,0:T(1,128)} %constant.2.clone.freq_ref, bf16[5120]{0:T(1024)(128)(2,1)} %g_ref.2, ...), custom_call_target="tpu_custom_call" | custom-call | tf_op jit(solution)/shard_map/attend/pallas_call | solution.py:163
  28.8 26.4 %combine.1.part_ref = f32[32,5120]{1,0:T(8,128)} custom-call(f32[128,32,128]{2,1,0:T(8,128)} %get-tuple-element.10.mix_ref, f32[32,128]{1,0:T(8,128)} %get-tuple-element.11.m_ref, f32[32,128]{1,0:T(8,128)} %get-tuple-element.12.l_ref, bf16[2048,5120]{1,0:T(8,128)(2,1)} %wo.1), custom_call_target="tpu_custom_call" | custom-call | tf_op jit(solution)/shard_map/combine/pallas_call | solution.py:292
  55.2 40.7 %hidden.1 = (f32[128,5120]{1,0:T(8,128)}, f32[16,5120]{1,0:T(8,128)}) custom-call(f32[32,5120]{1,0:T(8,128)} %combine.1.part_ref, bf16[256,5120]{1,0:T(8,128)(2,1)} %x_hbm.3, bf16[5120]{0:T(1024)(128)(2,1)} %g_ref.3, bf16[5120,7168]{1,0:T(8,128)(2,1)} %wg.1, bf16[5120,7168]{1,0:T(8,128)(2,1)} %wu.1, bf16[7168,5120]{1,0:T(8,128)(2,1)} %wd.1), custom_call_target="tpu_custom_call" | custom-call | tf_op jit(solution)/shard_map/hidden/pallas_call | solution.py:415
  95.9 43.8 %output.1 = bf16[256,5120]{1,0:T(8,128)(2,1)} custom-call(f32[128,5120]{1,0:T(8,128)} %get-tuple-element.13.part_ref, f32[16,5120]{1,0:T(8,128)} %get-tuple-element.14.hid_ref), custom_call_target="tpu_custom_call" | custom-call | tf_op jit(solution)/shard_map/output/pallas_call | solution.py:516
  139.7 3.4 %copy.18 = bf16[256,5120]{1,0:T(8,128)(2,1)} copy(bf16[256,5120]{1,0:T(8,128)(2,1)} %output.1) | data formatting | bytes 5242880

commit v4 on v3

--- a/solution.py
+++ b/solution.py
@@ -219,8 +219,6 @@
     partner = device(z, y, x, 1 - c)
     chips = [(y, x), (y, 1 - x), (1 - y, x), (1 - y, 1 - x)]
     weights = [pltpu.make_async_copy(wo.at[pl.ds(n * WN, WN)], wbuf.at[pl.ds(n * WN, WN)], sw.at[n]) for n in range(wo.shape[0] // WN)]
-    for cp in weights:
-        cp.start()
     greet([partner] + [device(z, b, a, c) for b, a in chips[1:]])
 
     st_own[0] = m_ref[...]
@@ -233,6 +231,8 @@
     stat1 = remote(st_own, st1, s1.at[4], r1.at[4], partner)
     stat1.start()
     for cp in first:
+        cp.start()
+    for cp in weights:
         cp.start()
     stat1.wait_recv()
     ma, mb = st_own[0], st1[0]
@@ -316,6 +316,7 @@
 
 
 GN = 256
+PIECES = 5
 KN = 1024
 HELD = 4096
 
@@ -340,56 +341,73 @@
     cx.start()
     loads = [gate_load(w, buf, sem, n) for n in range(wg.shape[0] // KN) for w, buf, sem in ((wg, gbuf, sg), (wu, ubuf, su))]
     loads += [down_load(n) for n in range(gates)]
-    for cp in loads:
-        cp.start()
     partner = device(z, y, x, 1 - c)
     zdev = device(1 - z, y, x, c)
-    z1, x1 = z + c * (1 - 2 * z), x + (1 - c) * (1 - 2 * x)
-    z2, x2 = z + (1 - c) * (1 - 2 * z), x + c * (1 - 2 * x)
-    dev1, dev2 = device(z1, y, x1, c), device(z2, y, x2, c)
-    greet([partner, dev1, dev2])
-    cz = remote(part_ref.at[pl.ds(16 * (1 - z), 16)], zb, sz, rz, zdev)
-    cz.start()
+    xdev = device(z, y, 1 - x, c)
+    dim = zb.shape[1]
+    step = dim // PIECES
+    cols = [pl.ds(p * step, step) for p in range(PIECES)]
+    greet([partner, zdev, xdev])
+    sums = [remote(part_ref.at[pl.ds(16 * (1 - z), 16), cols[p]], zb.at[:, cols[p]], sz.at[p], rz.at[p], zdev) for p in range(PIECES)]
+    for cp in sums:
+        cp.start()
+    for cp in loads:
+        cp.start()
     cx.wait()
-    cz.wait_recv()
-    own = part_ref[pl.ds(pl.multiple_of(16 * z, 16), 16), :]
-    hid = (x_ref[...].astype(jnp.float32) + (own + zb[...])).astype(jnp.bfloat16).astype(jnp.float32)
-    hid_ref[...] = hid
-    inv = lax.rsqrt(jnp.mean(hid * hid, axis=-1, keepdims=True) + NORM_EPS)
     slot = lambda zz, xx, cc: (xx * 2 + cc) * 2 + zz
     mine = slot(z, x, c)
-    hbuf[mine] = (hid * inv * g_ref[...].astype(jnp.float32).reshape(1, hid.shape[1])).astype(jnp.bfloat16).astype(jnp.float32)
-
-    def send(sl, dev, s, r, n):
-        cp = remote(hbuf.at[sl], hbuf.at[sl], s.at[n], r.at[n], dev)
+
+    def send(sl, p, dev, s, r, n):
+        cp = remote(hbuf.at[sl, :, cols[p]], hbuf.at[sl, :, cols[p]], s.at[n * PIECES + p], r.at[n * PIECES + p], dev)
         cp.start()
         return cp
 
-    a1 = send(mine, dev1, ss, rs, 0)
-    a2 = send(mine, dev2, ss, rs, 1)
-    d0 = send(mine, partner, sd, rd, 0)
-    a1.wait_recv()
-    s1 = slot(z1, x1, c)
-    a3 = send(s1, dev2, ss, rs, 2)
-    d1 = send(s1, partner, sd, rd, 1)
-    a2.wait_recv()
-    d2 = send(slot(z2, x2, c), partner, sd, rd, 2)
-    a3.wait_recv()
-    d3 = send(slot(1 - z, 1 - x, c), partner, sd, rd, 3)
-    for cp in (d0, d1, d2, d3):
-        cp.wait_recv()
-    for k in range(8):
-        h_s[pl.ds(16 * k, 16), :] = hbuf[k].astype(jnp.bfloat16)
-    for cp in (cz, a1, a2, a3, d0, d1, d2, d3):
+    over_z, over_x, over_c = {}, {}, {}
+    for p in range(PIECES):
+        sums[p].wait_recv()
+        own = part_ref[pl.ds(pl.multiple_of(16 * z, 16), 16), cols[p]] + zb[:, cols[p]]
+        hid = (x_ref[:, cols[p]].astype(jnp.float32) + own).astype(jnp.bfloat16).astype(jnp.float32)
+        hid_ref[:, cols[p]] = hid
+        hbuf[mine, :, cols[p]] = hid
+        over_z[p] = send(mine, p, zdev, ss, rs, 0)
+        over_x[0, p] = send(mine, p, xdev, ss, rs, 1)
+        over_c[0, p] = send(mine, p, partner, sd, rd, 0)
+    sz1, sx1, sd1 = slot(1 - z, x, c), slot(z, 1 - x, c), slot(1 - z, 1 - x, c)
+    for p in range(PIECES):
+        over_z[p].wait_recv()
+        over_x[1, p] = send(sz1, p, xdev, ss, rs, 2)
+        over_c[1, p] = send(sz1, p, partner, sd, rd, 1)
+    gain = g_ref[...].astype(jnp.float32).reshape(1, dim)
+
+    def norm(k):
+        hid = hbuf[k]
+        inv = lax.rsqrt(jnp.mean(hid * hid, axis=-1, keepdims=True) + NORM_EPS)
+        h_s[pl.ds(pl.multiple_of(16 * k, 16), 16), :] = (hid * inv * gain).astype(jnp.bfloat16)
+
+    norm(mine)
+    norm(sz1)
+    for p in range(PIECES):
+        over_x[0, p].wait_recv()
+        over_c[2, p] = send(sx1, p, partner, sd, rd, 2)
+    for p in range(PIECES):
+        over_x[1, p].wait_recv()
+        over_c[3, p] = send(sd1, p, partner, sd, rd, 3)
+    norm(sx1)
+    norm(sd1)
+    for n, (zz, xx) in enumerate(((z, x), (1 - z, x), (z, 1 - x), (1 - z, 1 - x))):
+        for p in range(PIECES):
+            over_c[n, p].wait_recv()
+        norm(slot(zz, xx, 1 - c))
+    for cp in sums + list(over_z.values()) + list(over_x.values()) + list(over_c.values()):
         cp.wait_send()
     up16 = lambda t: t.astype(jnp.bfloat16).astype(jnp.float32)
     for cp in loads[: len(loads) - gates]:
         cp.wait()
     for n in range(gates):
-        cols = slice(n * GN, (n + 1) * GN)
-        gate = up16(jnp.dot(h_s[...], gbuf[:, cols], preferred_element_type=jnp.float32))
-        up = up16(jnp.dot(h_s[...], ubuf[:, cols], preferred_element_type=jnp.float32))
-        act[:, cols] = (jax.nn.silu(gate) * up).astype(jnp.bfloat16)
+        part = slice(n * GN, (n + 1) * GN)
+        gate = up16(jnp.dot(h_s[...], gbuf[:, part], preferred_element_type=jnp.float32))
+        up = up16(jnp.dot(h_s[...], ubuf[:, part], preferred_element_type=jnp.float32))
+        act[:, part] = (jax.nn.silu(gate) * up).astype(jnp.bfloat16)
     held = dbuf.shape[1]
     rest = wd.shape[1] - held
     spare = gbuf.at[pl.ds(0, depth), pl.ds(0, rest)]
@@ -427,7 +445,7 @@
             pltpu.VMEM((dim, depth), bf16),
             pltpu.VMEM((depth, HELD), bf16),
             dma((dim // KN,)), dma((dim // KN,)), dma((depth // GN + 1,)),
-            dma, dma, dma, dma((3,)), dma((3,)), dma((4,)), dma((4,)),
+            dma, dma((PIECES,)), dma((PIECES,)), dma((3 * PIECES,)), dma((3 * PIECES,)), dma((4 * PIECES,)), dma((4 * PIECES,)),
         ],
         compiler_params=pltpu.CompilerParams(collective_id=1, has_side_effects=True, vmem_limit_bytes=VMEM_MOST),
         name="hidden",
@@ -525,7 +543,7 @@
             pltpu.VMEM((16, 16, dim), f32),
             dma((4,)), dma((4,)), dma((3,)), dma((3,)), dma((21,)), dma((21,)), dma((24,)), dma((24,)),
         ],
-        compiler_params=pltpu.CompilerParams(collective_id=2, has_side_effects=True, vmem_limit_bytes=VMEM_LIMIT),
+        compiler_params=pltpu.CompilerParams(collective_id=2, has_side_effects=True, vmem_limit_bytes=28 * 1024 * 1024),
         name="output",
     )(part, hid)
 

time: 143 us -> 133 us (0.930)
  Pallas kernels: 139 us -> 128 us
    pallas_call x1, Pallas kernels: 40.7 us -> 32.8 us  [hidden_call(): pl.pallas_call(hidden_kernel, out_shape=[jax.ShapeDtypeStruct((128, dim),...]
    pallas_call x1, Pallas kernels: 43.8 us -> 40.2 us  [output_call(): pl.pallas_call(output_kernel, out_shape=jax.ShapeDtypeStruct((256, dim),...]
    unnamed x1 -> x5, local copies, waits for them, and re-layouts: 3.4 us -> 4.2 us
where the time goes in v4:
time: 133 us; the launch traced here: 132 us
  Pallas kernels  128 us (96%)
  local copies, waits for them, and re-layouts  4.2 us (3%)
    pallas_call x1, Pallas kernels, output_call(): pl.pallas_call(output_kernel, out_shape=jax.ShapeDtypeStruct((256, dim),...  40.2 us
    pallas_call x1, Pallas kernels, hidden_call(): pl.pallas_call(hidden_kernel, out_shape=[jax.ShapeDtypeStruct((128, dim),...  32.8 us
    pallas_call x1, Pallas kernels, attend_call(): pl.pallas_call(attend_kernel, in_specs=[pl.BlockSpec(memory_space=pltpu.S...  28.1 us
    pallas_call x1, Pallas kernels, combine_call(): pl.pallas_call(combine_kernel, out_shape=jax.ShapeDtypeStruct((32, dim),...  26.4 us
    unnamed x5, local copies, waits for them, and re-layouts  4.2 us

profile of v4, /device:TPU:0, one launch (start us, length us, event | category | flops | bytes accessed | tf_op | source)
XLA Modules:
  0.0 132.4 jit_solution(11392165252674549296)
XLA Ops:
  0.6 28.1 %attend.1 = (bf16[256,128,128]{2,1,0:T(8,128)(2,1)}, bf16[256,128,128]{2,1,0:T(8,128)(2,1)}, f32[128,32,128]{2,1,0:T(8,128)}, f32[32,128]{1,0:T(8,128)}, f32[32,128]{1,0:T(8,128)}) custom-call(s32[256]{0:T(256)} %lens_ref.1, s32[256]{0:T(256)} %lens_ref.1, f32[1,128]{1,0:T(1,128)} %constant.2.clone.freq_ref, bf16[5120]{0:T(1024)(128)(2,1)} %g_ref.2, ...), custom_call_target="tpu_custom_call" | custom-call | tf_op jit(solution)/shard_map/attend/pallas_call | solution.py:163
  28.8 26.4 %combine.1.part_ref = f32[32,5120]{1,0:T(8,128)} custom-call(f32[128,32,128]{2,1,0:T(8,128)} %get-tuple-element.10.mix_ref, f32[32,128]{1,0:T(8,128)} %get-tuple-element.11.m_ref, f32[32,128]{1,0:T(8,128)} %get-tuple-element.12.l_ref, bf16[2048,5120]{1,0:T(8,128)(2,1)} %wo.1), custom_call_target="tpu_custom_call" | custom-call | tf_op jit(solution)/shard_map/combine/pallas_call | solution.py:292
  55.2 32.8 %hidden.1 = (f32[128,5120]{1,0:T(8,128)}, f32[16,5120]{1,0:T(8,128)}) custom-call(f32[32,5120]{1,0:T(8,128)} %combine.1.part_ref, bf16[256,5120]{1,0:T(8,128)(2,1)} %x_hbm.3, bf16[5120]{0:T(1024)(128)(2,1)} %g_ref.3, bf16[5120,7168]{1,0:T(8,128)(2,1)} %wg.1, bf16[5120,7168]{1,0:T(8,128)(2,1)} %wu.1, bf16[7168,5120]{1,0:T(8,128)(2,1)} %wd.1), custom_call_target="tpu_custom_call" | custom-call | tf_op jit(solution)/shard_map/hidden/pallas_call | solution.py:433
  88.0 0.0 copy-start
  88.0 1.7 %copy-done = f32[128,5120]{1,0:T(8,128)S(1)} copy-done((f32[128,5120]{1,0:T(8,128)S(1)}, f32[128,5120]{1,0:T(8,128)}, u32[]{:S(2)}) %copy-start) | copy-done | bytes 2621464
  89.7 0.0 copy-start.1
  89.7 1.0 copy-done.1
  90.7 40.2 %output.1 = bf16[256,5120]{1,0:T(8,128)(2,1)S(1)} custom-call(f32[128,5120]{1,0:T(8,128)S(1)} %copy-done, f32[16,5120]{1,0:T(8,128)S(1)} %copy-done.1), custom_call_target="tpu_custom_call" | custom-call | tf_op jit(solution)/shard_map/output/pallas_call | solution.py:534
  130.9 1.5 %copy.18 = bf16[256,5120]{1,0:T(8,128)(2,1)} copy(bf16[256,5120]{1,0:T(8,128)(2,1)S(1)} %output.1) | data formatting | bytes 5242880
Async XLA Ops:
  88.0 1.7 %copy-start = (f32[128,5120]{1,0:T(8,128)S(1)}, f32[128,5120]{1,0:T(8,128)}, u32[]{:S(2)}) copy-start(f32[128,5120]{1,0:T(8,128)} %get-tuple-element.13.part_ref) | copy-start | bytes 7864324
  89.7 1.0 copy-start.1

commit v5 on v4

--- a/solution.py
+++ b/solution.py
@@ -214,74 +214,90 @@
     return pltpu.make_async_remote_copy(src_ref=src, dst_ref=dst, send_sem=send, recv_sem=recv, device_id=dev, device_id_type=MESH)
 
 
-def combine_kernel(mix_ref, m_ref, l_ref, wo, part_ref, o_s, wbuf, sw, got1, st_own, st1, comb, stc, got2, st2, s1, r1, s2, r2):
+def combine_kernel(mix_ref, m_ref, l_ref, wo, part_ref, o_s, wbuf, sw, got1, st_own, st1, comb, stc, stn, got2, st2, s1, r1, s2, r2):
     z, y, x, c = coords()
     partner = device(z, y, x, 1 - c)
     chips = [(y, x), (y, 1 - x), (1 - y, x), (1 - y, 1 - x)]
-    weights = [pltpu.make_async_copy(wo.at[pl.ds(n * WN, WN)], wbuf.at[pl.ds(n * WN, WN)], sw.at[n]) for n in range(wo.shape[0] // WN)]
-    greet([partner] + [device(z, b, a, c) for b, a in chips[1:]])
+    y1, x1 = y + c * (1 - 2 * y), x + (1 - c) * (1 - 2 * x)
+    y2, x2 = y + (1 - c) * (1 - 2 * y), x + c * (1 - 2 * x)
+    dev1, dev2 = device(z, y1, x1, c), device(z, y2, x2, c)
+    k1, k2 = 1 + c, 2 - c
+    greet([partner, dev1, dev2])
 
     st_own[0] = m_ref[...]
     st_own[1] = l_ref[...]
-    first = []
-    for k in (1, 2, 3, 0):
+    stat1 = remote(st_own, st1, s1.at[4], r1.at[4], partner)
+    stat1.start()
+    first = {}
+    for k in (3, 1, 2, 0):
         b, a = chips[k]
         start = 16 * (b * 4 + a * 2 + 1 - c)
-        first.append(remote(mix_ref.at[pl.ds(start, 16)], got1.at[k], s1.at[k], r1.at[k], partner))
-    stat1 = remote(st_own, st1, s1.at[4], r1.at[4], partner)
-    stat1.start()
-    for cp in first:
-        cp.start()
+        first[k] = remote(mix_ref.at[pl.ds(start, 16)], got1.at[k], s1.at[k], r1.at[k], partner)
+        first[k].start()
+    weights = [pltpu.make_async_copy(wo.at[pl.ds(n * WN, WN)], wbuf.at[pl.ds(n * WN, WN)], sw.at[n]) for n in range(wo.shape[0] // WN)]
+
+    def merge(pa, pb):
+        m = jnp.maximum(pa[0], pb[0])
+        fa, fb = jnp.exp(pa[0] - m), jnp.exp(pb[0] - m)
+        return m, pa[1] * fa + pb[1] * fb, fa, fb
+
+    def turned(f, b, a):
+        return pltpu.roll(f, (128 - 16 * (b * 4 + a * 2 + c)) % 128, 1)
+
+    stat1.wait_recv()
+    m, l, fa, fb = merge((st_own[0], st_own[1]), (st1[0], st1[1]))
+    stc[0] = m
+    stc[1] = l
+    stat2 = remote(stc, st2.at[0], s2.at[3], r2.at[3], dev1)
+    stat2.start()
+
+    def pair_sum(k):
+        b, a = chips[k]
+        ga, gb = turned(fa, b, a), turned(fb, b, a)
+        first[k].wait_recv()
+        for j in range(16):
+            comb[k, j] = mix_ref[16 * (b * 4 + a * 2 + c) + j] * ga[:, j : j + 1] + got1[k, j] * gb[:, j : j + 1]
+
+    def hop(src, dst, dev):
+        cp = remote(comb.at[src], got2.at[dst], s2.at[dst], r2.at[dst], dev)
+        cp.start()
+        return cp
+
+    pair_sum(3)
+    far = hop(3, 0, dev1)
+    pair_sum(1)
+    pair_sum(2)
+    direct = hop(k1, 1, dev1)
     for cp in weights:
         cp.start()
-    stat1.wait_recv()
-    ma, mb = st_own[0], st1[0]
-    mg = jnp.maximum(ma, mb)
-    fa, fb = jnp.exp(ma - mg), jnp.exp(mb - mg)
-    stc[0] = mg
-    stc[1] = st_own[1] * fa + st1[1] * fb
-    second = {}
-    stats2 = {}
-    for k in (1, 2, 3):
-        b, a = chips[k]
-        stats2[k] = remote(stc, st2.at[k - 1], s2.at[3 + k - 1], r2.at[3 + k - 1], device(z, b, a, c))
-        stats2[k].start()
-    for n, k in enumerate((1, 2, 3, 0)):
-        b, a = chips[k]
-        block = b * 4 + a * 2 + c
-        back = (128 - 16 * block) % 128
-        ga, gb = pltpu.roll(fa, back, 1), pltpu.roll(fb, back, 1)
-        first[n].wait_recv()
-        for j in range(16):
-            comb[k, j] = mix_ref[16 * block + j] * ga[:, j : j + 1] + got1[k, j] * gb[:, j : j + 1]
-        if k:
-            second[k] = remote(comb.at[k], got2.at[k - 1], s2.at[k - 1], r2.at[k - 1], device(z, b, a, c))
-            second[k].start()
-    for k in (1, 2, 3):
-        stats2[k].wait_recv()
-    ms = [stc[0]] + [st2[k, 0] for k in range(3)]
-    ls = [stc[1]] + [st2[k, 1] for k in range(3)]
-    mg = jnp.maximum(jnp.maximum(ms[0], ms[1]), jnp.maximum(ms[2], ms[3]))
-    fs = [jnp.exp(m - mg) for m in ms]
-    total = ls[0] * fs[0] + ls[1] * fs[1] + ls[2] * fs[2] + ls[3] * fs[3]
-    block = y * 4 + x * 2 + c
-    back = (128 - 16 * block) % 128
-    fs = [pltpu.roll(f, back, 1) for f in fs]
-    total = pltpu.roll(total, back, 1)
-    for k in (1, 2, 3):
-        second[k].wait_recv()
+    pair_sum(0)
+    stat2.wait_recv()
+    m, l, fa, fb = merge((m, l), (st2[0, 0], st2[0, 1]))
+    stn[0] = m
+    stn[1] = l
+    stat3 = remote(stn, st2.at[1], s2.at[4], r2.at[4], dev2)
+    stat3.start()
+    ga, gb = turned(fa, y2, x2), turned(fb, y2, x2)
+    far.wait_recv()
     for j in range(16):
-        acc = comb[0, j] * fs[0][:, j : j + 1]
-        for k in (1, 2, 3):
-            acc = acc + got2[k - 1, j] * fs[k][:, j : j + 1]
-        o_s[32 * j : 32 * j + 32, :] = acc / total[:, j : j + 1]
+        comb[4, j] = comb[k2, j] * ga[:, j : j + 1] + got2[0, j] * gb[:, j : j + 1]
+    second = hop(4, 2, dev2)
+    stat3.wait_recv()
+    _, l, na, nb = merge((m, l), (st2[1, 0], st2[1, 1]))
+    fa, fb, nb, l = turned(fa * na, y, x), turned(fb * na, y, x), turned(nb, y, x), turned(l, y, x)
+    direct.wait_recv()
+    second.wait_recv()
+    for j in range(16):
+        at = slice(j, j + 1)
+        acc = comb[0, j] * fa[:, at] + got2[1, j] * fb[:, at] + got2[2, j] * nb[:, at]
+        o_s[32 * j : 32 * j + 32, :] = acc / l[:, at]
     o = jnp.concatenate([o_s[pl.ds(h, 32, stride=16), :].astype(jnp.bfloat16) for h in range(16)], axis=1)
     for cp in weights:
         cp.wait()
     for n in range(wo.shape[1] // WN):
         cols = slice(n * WN, (n + 1) * WN)
         part_ref[:, cols] = jnp.dot(o, wbuf[:, cols], preferred_element_type=jnp.float32)
-    for cp in first + [stat1] + [stats2[k] for k in stats2] + [second[k] for k in second]:
+    for cp in list(first.values()) + [stat1, stat2, stat3, far, direct, second]:
         cp.wait_send()
 
 
@@ -301,14 +317,15 @@
             pltpu.VMEM((4, 16, 32, 128), f32),
             pltpu.VMEM((2, 32, 128), f32),
             pltpu.VMEM((2, 32, 128), f32),
-            pltpu.VMEM((4, 16, 32, 128), f32),
+            pltpu.VMEM((5, 16, 32, 128), f32),
+            pltpu.VMEM((2, 32, 128), f32),
             pltpu.VMEM((2, 32, 128), f32),
             pltpu.VMEM((3, 16, 32, 128), f32),
-            pltpu.VMEM((3, 2, 32, 128), f32),
+            pltpu.VMEM((2, 2, 32, 128), f32),
             pltpu.SemaphoreType.DMA((5,)),
             pltpu.SemaphoreType.DMA((5,)),
-            pltpu.SemaphoreType.DMA((6,)),
-            pltpu.SemaphoreType.DMA((6,)),
+            pltpu.SemaphoreType.DMA((5,)),
+            pltpu.SemaphoreType.DMA((5,)),
         ],
         compiler_params=pltpu.CompilerParams(collective_id=0, has_side_effects=True, vmem_limit_bytes=VMEM_LIMIT),
         name="combine",
@@ -460,35 +477,48 @@
     partner = device(z, y, x, 1 - c)
     chips = [(z, x), (z, 1 - x), (1 - z, x), (1 - z, 1 - x)]
     near = [device(z, y, 1 - x, c), device(z, 1 - y, x, c), device(1 - z, y, x, c)]
-    greet([partner] + near + [device(1 - z, y, 1 - x, c)])
+    greet([partner] + near)
     slot = lambda zz, xx, cc: (xx * 2 + cc) * 2 + zz
     rows16 = lambda s: pl.ds(pl.multiple_of(16 * s, 16), 16)
-    order = (3, 1, 2, 0)
+    cols = [pl.ds(*color) for color in COLORS]
+    z1, x1 = z + c * (1 - 2 * z), x + (1 - c) * (1 - 2 * x)
+    z2, x2 = z + (1 - c) * (1 - 2 * z), x + c * (1 - 2 * x)
+    dev1, dev2 = device(z1, y, x1, c), device(z2, y, x2, c)
+    k1, k2 = 1 + c, 2 - c
+    links, locals_, sums = {}, {}, []
     first = {}
-    for k in order:
-        zz, xx = chips[k]
-        first[k] = remote(part_ref.at[rows16(slot(zz, xx, 1 - c))], got1.at[k], s1.at[k], r1.at[k], partner)
-        first[k].start()
-    second = {}
-    for k in order:
-        zz, xx = chips[k]
-        first[k].wait_recv()
-        acc[k] = part_ref[rows16(slot(zz, xx, c)), :] + got1[k]
-        if k:
-            second[k] = remote(acc.at[k], got2.at[k - 1], s2.at[k - 1], r2.at[k - 1], device(zz, y, xx, c))
-            second[k].start()
-    for k in (1, 2, 3):
-        second[k].wait_recv()
-    total = (acc[0] + got2[0]) + (got2[1] + got2[2])
+    for p in range(3):
+        for k in (3, 1, 2, 0):
+            zz, xx = chips[k]
+            n = 4 * p + k
+            first[k, p] = remote(part_ref.at[rows16(slot(zz, xx, 1 - c)), cols[p]], got1.at[k, :, cols[p]], s1.at[n], r1.at[n], partner)
+            first[k, p].start()
+
+    def hop(src, dst, p, dev):
+        n = 3 * p + dst
+        cp = remote(acc.at[src, :, cols[p]], got2.at[dst, :, cols[p]], s2.at[n], r2.at[n], dev)
+        cp.start()
+        sums.append(cp)
+        return cp
+
+    far, direct, second = {}, {}, {}
+    for p in range(3):
+        for k in (3, 1, 2, 0):
+            zz, xx = chips[k]
+            first[k, p].wait_recv()
+            acc[k, :, cols[p]] = part_ref[rows16(slot(zz, xx, c)), cols[p]] + got1[k, :, cols[p]]
+        far[p] = hop(3, 0, p, dev1)
+        direct[p] = hop(k1, 1, p, dev1)
+    for p in range(3):
+        far[p].wait_recv()
+        acc[4, :, cols[p]] = acc[k2, :, cols[p]] + got2[0, :, cols[p]]
+        second[p] = hop(4, 2, p, dev2)
     mine = y * 8 + slot(z, x, c)
-    ybuf[mine] = (hid_ref[...] + total).astype(jnp.bfloat16).astype(jnp.float32)
 
     def shard(mask):
         zz, yy, xx = flip(z, mask & 4), flip(y, mask & 2), flip(x, mask & 1)
         return yy * 8 + slot(zz, xx, c)
 
-    links, locals_ = {}, {}
-
     def piece(mask, k):
         return ybuf.at[shard(mask), :, pl.ds(*COLORS[k])]
 
@@ -505,10 +535,14 @@
         locals_[k, mask] = cp
 
     turn = lambda k: [(k + i) % 3 for i in range(3)]
-    for i in range(3):
-        for k in range(3):
+    for k in range(3):
+        direct[k].wait_recv()
+        near_sum = acc[0, :, cols[k]] + got2[1, :, cols[k]]
+        second[k].wait_recv()
+        total = near_sum + got2[2, :, cols[k]]
+        ybuf[mine, :, cols[k]] = (hid_ref[:, cols[k]] + total).astype(jnp.bfloat16).astype(jnp.float32)
+        for i in range(3):
             push(0, k, turn(k)[i])
-    for k in range(3):
         across(0, k)
     for level in ((0,), (1,), (0, 1), (2,), (0, 2), (1, 2), (0, 1, 2)):
         for k in range(3):
@@ -522,7 +556,7 @@
         cp.wait_recv()
     for s in range(16):
         y_ref[pl.ds(16 * s, 16), :] = ybuf[s].astype(jnp.bfloat16)
-    for cp in list(first.values()) + list(second.values()) + list(links.values()) + list(locals_.values()):
+    for cp in list(first.values()) + sums + list(links.values()) + list(locals_.values()):
         cp.wait_send()
 
 
@@ -538,10 +572,10 @@
         out_specs=vm,
         scratch_shapes=[
             pltpu.VMEM((4, 16, dim), f32),
-            pltpu.VMEM((4, 16, dim), f32),
+            pltpu.VMEM((5, 16, dim), f32),
             pltpu.VMEM((3, 16, dim), f32),
             pltpu.VMEM((16, 16, dim), f32),
-            dma((4,)), dma((4,)), dma((3,)), dma((3,)), dma((21,)), dma((21,)), dma((24,)), dma((24,)),
+            dma((12,)), dma((12,)), dma((9,)), dma((9,)), dma((21,)), dma((21,)), dma((24,)), dma((24,)),
         ],
         compiler_params=pltpu.CompilerParams(collective_id=2, has_side_effects=True, vmem_limit_bytes=28 * 1024 * 1024),
         name="output",

time: 133 us -> 125 us (0.940)
  Pallas kernels: 128 us -> 120 us
    pallas_call x1, Pallas kernels: 40.2 us -> 35.3 us  [output_call(): pl.pallas_call(output_kernel, out_shape=jax.ShapeDtypeStruct((256, dim),...]
    pallas_call x1, Pallas kernels: 26.4 us -> 23 us  [combine_call(): pl.pallas_call(combine_kernel, out_shape=jax.ShapeDtypeStruct((32, dim),...]
where the time goes in v5:
time: 125 us; the launch traced here: 124 us
  Pallas kernels  120 us (96%)
  local copies, waits for them, and re-layouts  4.2 us (3%)
    pallas_call x1, Pallas kernels, output_call(): pl.pallas_call(output_kernel, out_shape=jax.ShapeDtypeStruct((256, dim),...  35.3 us
    pallas_call x1, Pallas kernels, hidden_call(): pl.pallas_call(hidden_kernel, out_shape=[jax.ShapeDtypeStruct((128, dim),...  33.1 us
    pallas_call x1, Pallas kernels, attend_call(): pl.pallas_call(attend_kernel, in_specs=[pl.BlockSpec(memory_space=pltpu.S...  28.1 us
    pallas_call x1, Pallas kernels, combine_call(): pl.pallas_call(combine_kernel, out_shape=jax.ShapeDtypeStruct((32, dim),...  23 us
    unnamed x5, local copies, waits for them, and re-layouts  4.2 us

profile of v5, /device:TPU:0, one launch (start us, length us, event | category | flops | bytes accessed | tf_op | source)
XLA Modules:
  0.0 124.4 jit_solution(8856970144752060526)
XLA Ops:
  0.6 28.1 %attend.1 = (bf16[256,128,128]{2,1,0:T(8,128)(2,1)}, bf16[256,128,128]{2,1,0:T(8,128)(2,1)}, f32[128,32,128]{2,1,0:T(8,128)}, f32[32,128]{1,0:T(8,128)}, f32[32,128]{1,0:T(8,128)}) custom-call(s32[256]{0:T(256)} %lens_ref.1, s32[256]{0:T(256)} %lens_ref.1, f32[1,128]{1,0:T(1,128)} %constant.2.clone.freq_ref, bf16[5120]{0:T(1024)(128)(2,1)} %g_ref.2, ...), custom_call_target="tpu_custom_call" | custom-call | tf_op jit(solution)/shard_map/attend/pallas_call | solution.py:163
  28.8 23.0 %combine.1.part_ref = f32[32,5120]{1,0:T(8,128)} custom-call(f32[128,32,128]{2,1,0:T(8,128)} %get-tuple-element.10.mix_ref, f32[32,128]{1,0:T(8,128)} %get-tuple-element.11.m_ref, f32[32,128]{1,0:T(8,128)} %get-tuple-element.12.l_ref, bf16[2048,5120]{1,0:T(8,128)(2,1)} %wo.1), custom_call_target="tpu_custom_call" | custom-call | tf_op jit(solution)/shard_map/combine/pallas_call | solution.py:308
  51.7 33.1 %hidden.1 = (f32[128,5120]{1,0:T(8,128)}, f32[16,5120]{1,0:T(8,128)}) custom-call(f32[32,5120]{1,0:T(8,128)} %combine.1.part_ref, bf16[256,5120]{1,0:T(8,128)(2,1)} %x_hbm.3, bf16[5120]{0:T(1024)(128)(2,1)} %g_ref.3, bf16[5120,7168]{1,0:T(8,128)(2,1)} %wg.1, bf16[5120,7168]{1,0:T(8,128)(2,1)} %wu.1, bf16[7168,5120]{1,0:T(8,128)(2,1)} %wd.1), custom_call_target="tpu_custom_call" | custom-call | tf_op jit(solution)/shard_map/hidden/pallas_call | solution.py:450
  84.8 0.0 copy-start
  84.9 1.7 %copy-done = f32[128,5120]{1,0:T(8,128)S(1)} copy-done((f32[128,5120]{1,0:T(8,128)S(1)}, f32[128,5120]{1,0:T(8,128)}, u32[]{:S(2)}) %copy-start) | copy-done | bytes 2621464
  86.6 0.0 copy-start.1
  86.6 1.0 copy-done.1
  87.6 35.3 %output.1 = bf16[256,5120]{1,0:T(8,128)(2,1)S(1)} custom-call(f32[128,5120]{1,0:T(8,128)S(1)} %copy-done, f32[16,5120]{1,0:T(8,128)S(1)} %copy-done.1), custom_call_target="tpu_custom_call" | custom-call | tf_op jit(solution)/shard_map/output/pallas_call | solution.py:568
  122.9 1.5 %copy.18 = bf16[256,5120]{1,0:T(8,128)(2,1)} copy(bf16[256,5120]{1,0:T(8,128)(2,1)S(1)} %output.1) | data formatting | bytes 5242880
Async XLA Ops:
  84.8 1.7 %copy-start = (f32[128,5120]{1,0:T(8,128)S(1)}, f32[128,5120]{1,0:T(8,128)}, u32[]{:S(2)}) copy-start(f32[128,5120]{1,0:T(8,128)} %get-tuple-element.13.part_ref) | copy-start | bytes 7864324
  86.6 1.0 copy-start.1

commit v6 on v5

--- a/solution.py
+++ b/solution.py
@@ -20,8 +20,8 @@
 PAIRS = 16
 
 
-def attend_kernel(lens_s, lens_ref, freq_ref, g_ref, x_hbm, wq, wk, wv, kc, vc, ko, vo, mix_ref, m_ref, l_ref,
-                  xb, u, wbuf, q_s, kn_s, vn_s, cos_s, sin_s, kbuf, vbuf, sx, sw, sk, sv, tk, tv):
+def attend_kernel(lens_s, lens_ref, freq_ref, g_ref, x_hbm, wq, wk, wv, kc, vc, ko, vo, mix_out, st_ref,
+                  mix_ref, smix, xb, u, wbuf, q_s, kn_s, vn_s, cos_s, sin_s, kbuf, vbuf, sx, sw, sk, sv, tk, tv):
     rows, dim = xb.shape
     nq, nk, nv = wq.shape[1] // WN, wk.shape[1] // WN, wv.shape[1] // WN
     blocks = kc.shape[0] // RB
@@ -44,6 +44,10 @@
     def store(n):
         r, t = pl.ds(n * RB, RB), n % RING
         return pltpu.make_async_copy(kbuf.at[t], ko.at[r], tk.at[t]), pltpu.make_async_copy(vbuf.at[t], vo.at[r], tv.at[t])
+
+    def mixed(n):
+        r = pl.ds(n * (RB // 2), RB // 2)
+        return pltpu.make_async_copy(mix_ref.at[r], mix_out.at[r], smix.at[n])
 
     eye = lax.broadcasted_iota(jnp.int32, (rows, rows), 0) == lax.broadcasted_iota(jnp.int32, (rows, rows), 1)
     lens_f = lens_ref[...].astype(jnp.float32).reshape(1, rows)
@@ -53,8 +57,7 @@
     cos_s[...] = jnp.cos(angles)
     sin_a = jnp.sin(angles)
     sin_s[...] = jnp.where(half, -sin_a, sin_a)
-    m_ref[...] = jnp.zeros_like(m_ref)
-    l_ref[...] = jnp.zeros_like(l_ref)
+    st_ref[...] = jnp.zeros_like(st_ref)
 
     cx.wait()
     gain = g_ref[...].astype(jnp.float32).reshape(1, dim)
@@ -105,7 +108,7 @@
             cp.wait()
 
         def group(g, carry, n=n, slot=slot):
-            m_all, l_all = m_ref[...], l_ref[...]
+            m_all, l_all = st_ref[0], st_ref[1]
             for j in range(PAIRS):
                 local = g * PAIRS + j
                 pair = n * (RB // 2) + local
@@ -135,13 +138,14 @@
                 mix_ref[pair, 16:] = jnp.dot(w[16:, 128:].astype(jnp.bfloat16), vs[1], preferred_element_type=jnp.float32)
                 m_all = jnp.where(lane == pair, m, m_all)
                 l_all = jnp.where(lane == pair, l, l_all)
-            m_ref[...] = m_all
-            l_ref[...] = l_all
+            st_ref[0] = m_all
+            st_ref[1] = l_all
             return carry
 
         lax.fori_loop(0, RB // 2 // PAIRS, group, 0)
         for cp in store(n):
             cp.start()
+        mixed(n).start()
         if n >= 1 and n - 1 + RING < blocks:
             for cp in store(n - 1):
                 cp.wait()
@@ -150,6 +154,8 @@
     for n in range(blocks - RING, blocks):
         for cp in store(n):
             cp.wait()
+    for n in range(blocks):
+        mixed(n).wait()
 
 
 def attend_call(seq_lens, freq, g_attn, x_tok, wq, wk, wv, k2, v2):
@@ -163,15 +169,16 @@
     return pl.pallas_call(
         attend_kernel,
         in_specs=[pl.BlockSpec(memory_space=pltpu.SMEM), vm, vm, vm] + [hbm] * 6,
-        out_specs=[hbm, hbm, vm, vm, vm],
+        out_specs=[hbm, hbm, hbm, vm],
         out_shape=[
             jax.ShapeDtypeStruct(k2.shape, bf16),
             jax.ShapeDtypeStruct(v2.shape, bf16),
             jax.ShapeDtypeStruct((batch // 2, 32, 128), f32),
-            jax.ShapeDtypeStruct((32, 128), f32),
-            jax.ShapeDtypeStruct((32, 128), f32),
+            jax.ShapeDtypeStruct((2, 32, 128), f32),
         ],
         scratch_shapes=[
+            pltpu.VMEM((batch // 2, 32, 128), f32),
+            dma((batch // RB,)),
             pltpu.VMEM((rows, dim), bf16),
             pltpu.VMEM((rows, dim), bf16),
             pltpu.VMEM((chunks, dim, WN), bf16),
@@ -214,7 +221,7 @@
     return pltpu.make_async_remote_copy(src_ref=src, dst_ref=dst, send_sem=send, recv_sem=recv, device_id=dev, device_id_type=MESH)
 
 
-def combine_kernel(mix_ref, m_ref, l_ref, wo, part_ref, o_s, wbuf, sw, got1, st_own, st1, comb, stc, stn, got2, st2, s1, r1, s2, r2):
+def combine_kernel(mix_hbm, st_own, wo, part_ref, own, so, o_s, wbuf, sw, got1, st1, comb, stc, stn, got2, st2, s1, r1, s2, r2):
     z, y, x, c = coords()
     partner = device(z, y, x, 1 - c)
     chips = [(y, x), (y, 1 - x), (1 - y, x), (1 - y, 1 - x)]
@@ -222,18 +229,20 @@
     y2, x2 = y + (1 - c) * (1 - 2 * y), x + c * (1 - 2 * x)
     dev1, dev2 = device(z, y1, x1, c), device(z, y2, x2, c)
     k1, k2 = 1 + c, 2 - c
+    kept = {}
+    for k in (3, 1, 2, 0):
+        b, a = chips[k]
+        kept[k] = pltpu.make_async_copy(mix_hbm.at[pl.ds(16 * (b * 4 + a * 2 + c), 16)], own.at[k], so.at[k])
     greet([partner, dev1, dev2])
-
-    st_own[0] = m_ref[...]
-    st_own[1] = l_ref[...]
     stat1 = remote(st_own, st1, s1.at[4], r1.at[4], partner)
     stat1.start()
     first = {}
     for k in (3, 1, 2, 0):
         b, a = chips[k]
         start = 16 * (b * 4 + a * 2 + 1 - c)
-        first[k] = remote(mix_ref.at[pl.ds(start, 16)], got1.at[k], s1.at[k], r1.at[k], partner)
+        first[k] = remote(mix_hbm.at[pl.ds(start, 16)], got1.at[k], s1.at[k], r1.at[k], partner)
         first[k].start()
+        kept[k].start()
     weights = [pltpu.make_async_copy(wo.at[pl.ds(n * WN, WN)], wbuf.at[pl.ds(n * WN, WN)], sw.at[n]) for n in range(wo.shape[0] // WN)]
 
     def merge(pa, pb):
@@ -254,9 +263,10 @@
     def pair_sum(k):
         b, a = chips[k]
         ga, gb = turned(fa, b, a), turned(fb, b, a)
+        kept[k].wait()
         first[k].wait_recv()
         for j in range(16):
-            comb[k, j] = mix_ref[16 * (b * 4 + a * 2 + c) + j] * ga[:, j : j + 1] + got1[k, j] * gb[:, j : j + 1]
+            comb[k, j] = own[k, j] * ga[:, j : j + 1] + got1[k, j] * gb[:, j : j + 1]
 
     def hop(src, dst, dev):
         cp = remote(comb.at[src], got2.at[dst], s2.at[dst], r2.at[dst], dev)
@@ -301,21 +311,22 @@
         cp.wait_send()
 
 
-def combine_call(mix, m, l, wo):
+def combine_call(mix, stat, wo):
     vm = pl.BlockSpec(memory_space=pltpu.VMEM)
     f32 = jnp.float32
     depth, dim = wo.shape
     return pl.pallas_call(
         combine_kernel,
         out_shape=jax.ShapeDtypeStruct((32, dim), f32),
-        in_specs=[vm, vm, vm, pl.BlockSpec(memory_space=pl.ANY)],
+        in_specs=[pl.BlockSpec(memory_space=pl.ANY), vm, pl.BlockSpec(memory_space=pl.ANY)],
         out_specs=vm,
         scratch_shapes=[
+            pltpu.VMEM((4, 16, 32, 128), f32),
+            pltpu.SemaphoreType.DMA((4,)),
             pltpu.VMEM((512, 128), f32),
             pltpu.VMEM((depth, dim), jnp.bfloat16),
             pltpu.SemaphoreType.DMA((depth // WN,)),
             pltpu.VMEM((4, 16, 32, 128), f32),
-            pltpu.VMEM((2, 32, 128), f32),
             pltpu.VMEM((2, 32, 128), f32),
             pltpu.VMEM((5, 16, 32, 128), f32),
             pltpu.VMEM((2, 32, 128), f32),
@@ -329,7 +340,7 @@
         ],
         compiler_params=pltpu.CompilerParams(collective_id=0, has_side_effects=True, vmem_limit_bytes=VMEM_LIMIT),
         name="combine",
-    )(mix, m, l, wo)
+    )(mix, stat, wo)
 
 
 GN = 256
@@ -338,7 +349,7 @@
 HELD = 4096
 
 
-def hidden_kernel(part_ref, x_hbm, g_ref, wg, wu, wd, down_ref, hid_ref, x_ref, zb, hbuf, h_s, act, gbuf, ubuf, dbuf,
+def hidden_kernel(part_hbm, x_hbm, g_ref, wg, wu, wd, down_hbm, hid_ref, part_s, down_s, sp, sdo, x_ref, zb, hbuf, h_s, act, gbuf, ubuf, dbuf,
                   sg, su, sdw, sx, sz, rz, ss, rs, sd, rd):
     z, y, x, c = coords()
     depth = act.shape[1]
@@ -356,6 +367,8 @@
     at = pl.multiple_of(32 * (y * 4 + x * 2 + c) + 16 * z, 16)
     cx = pltpu.make_async_copy(x_hbm.at[pl.ds(at, 16)], x_ref, sx)
     cx.start()
+    cp_own = pltpu.make_async_copy(part_hbm.at[pl.ds(pl.multiple_of(16 * z, 16), 16)], part_s, sp)
+    cp_own.start()
     loads = [gate_load(w, buf, sem, n) for n in range(wg.shape[0] // KN) for w, buf, sem in ((wg, gbuf, sg), (wu, ubuf, su))]
     loads += [down_load(n) for n in range(gates)]
     partner = device(z, y, x, 1 - c)
@@ -365,12 +378,13 @@
     step = dim // PIECES
     cols = [pl.ds(p * step, step) for p in range(PIECES)]
     greet([partner, zdev, xdev])
-    sums = [remote(part_ref.at[pl.ds(16 * (1 - z), 16), cols[p]], zb.at[:, cols[p]], sz.at[p], rz.at[p], zdev) for p in range(PIECES)]
+    sums = [remote(part_hbm.at[pl.ds(16 * (1 - z), 16), cols[p]], zb.at[:, cols[p]], sz.at[p], rz.at[p], zdev) for p in range(PIECES)]
     for cp in sums:
         cp.start()
     for cp in loads:
         cp.start()
     cx.wait()
+    cp_own.wait()
     slot = lambda zz, xx, cc: (xx * 2 + cc) * 2 + zz
     mine = slot(z, x, c)
 
@@ -382,7 +396,7 @@
     over_z, over_x, over_c = {}, {}, {}
     for p in range(PIECES):
         sums[p].wait_recv()
-        own = part_ref[pl.ds(pl.multiple_of(16 * z, 16), 16), cols[p]] + zb[:, cols[p]]
+        own = part_s[:, cols[p]] + zb[:, cols[p]]
         hid = (x_ref[:, cols[p]].astype(jnp.float32) + own).astype(jnp.bfloat16).astype(jnp.float32)
         hid_ref[:, cols[p]] = hid
         hbuf[mine, :, cols[p]] = hid
@@ -425,6 +439,10 @@
         gate = up16(jnp.dot(h_s[...], gbuf[:, part], preferred_element_type=jnp.float32))
         up = up16(jnp.dot(h_s[...], ubuf[:, part], preferred_element_type=jnp.float32))
         act[:, part] = (jax.nn.silu(gate) * up).astype(jnp.bfloat16)
+    def out(n):
+        r = pl.ds(n * WN, WN)
+        return pltpu.make_async_copy(down_s.at[:, r], down_hbm.at[:, r], sdo.at[n])
+
     held = dbuf.shape[1]
     rest = wd.shape[1] - held
     spare = gbuf.at[pl.ds(0, depth), pl.ds(0, rest)]
@@ -436,7 +454,10 @@
         if n * WN == held:
             last.wait()
         wide = dbuf[:, n * WN : (n + 1) * WN] if n * WN < held else gbuf[:depth, n * WN - held : (n + 1) * WN - held]
-        down_ref[:, n * WN : (n + 1) * WN] = jnp.dot(act[...], wide, preferred_element_type=jnp.float32)
+        down_s[:, n * WN : (n + 1) * WN] = jnp.dot(act[...], wide, preferred_element_type=jnp.float32)
+        out(n).start()
+    for n in range(downs):
+        out(n).wait()
 
 
 def hidden_call(part, x_tok, g, wg, wu, wd, ways):
@@ -450,9 +471,13 @@
     return pl.pallas_call(
         hidden_kernel,
         out_shape=[jax.ShapeDtypeStruct((128, dim), f32), jax.ShapeDtypeStruct((16, dim), f32)],
-        in_specs=[vm, hbm, vm, hbm, hbm, hbm],
-        out_specs=[vm, vm],
+        in_specs=[hbm, hbm, vm, hbm, hbm, hbm],
+        out_specs=[hbm, vm],
         scratch_shapes=[
+            pltpu.VMEM((16, dim), f32),
+            pltpu.VMEM((128, dim), f32),
+            dma,
+            dma((dim // WN,)),
             pltpu.VMEM((16, dim), bf16),
             pltpu.VMEM((16, dim), f32),
             pltpu.VMEM((8, 16, dim), f32),
@@ -594,8 +619,8 @@
         freq = ROPE_BASE ** (np.arange(head_dim // 2, dtype=np.float64) * (-2.0 / head_dim))
         freq = jnp.asarray(np.concatenate([freq, freq])[None].astype(np.float32))
         flat = (batch, seq_blk * kv_loc, head_dim)
-        k_out, v_out, mix, m, l = attend_call(seq_lens, freq, g_attn, x_tok, wq_loc, wk_loc, wv_loc, k_blk.reshape(flat), v_blk.reshape(flat))
-        part = combine_call(mix, m, l, wo_loc)
+        k_out, v_out, mix, stat = attend_call(seq_lens, freq, g_attn, x_tok, wq_loc, wk_loc, wv_loc, k_blk.reshape(flat), v_blk.reshape(flat))
+        part = combine_call(mix, stat, wo_loc)
         down, hid = hidden_call(part, x_tok, g_mlp, wg_loc, wu_loc, wd_loc, 4)
         y_out = output_call(down, hid)
         return y_out, k_out.reshape(k_blk.shape), v_out.reshape(v_blk.shape)

time: 125 us -> 124 us (level)
  Pallas kernels: 120 us -> 118 us
where the time goes in v6:
time: 124 us; the launch traced here: 123 us
  Pallas kernels  118 us (95%)
  local copies, waits for them, and re-layouts  4.2 us (3%)
    pallas_call x1, Pallas kernels, output_call(): pl.pallas_call(output_kernel, out_shape=jax.ShapeDtypeStruct((256, dim),...  35.4 us
    pallas_call x1, Pallas kernels, hidden_call(): pl.pallas_call(hidden_kernel, out_shape=[jax.ShapeDtypeStruct((128, dim),...  32.8 us
    pallas_call x1, Pallas kernels, attend_call(): pl.pallas_call(attend_kernel, in_specs=[pl.BlockSpec(memory_space=pltpu.S...  28 us
    pallas_call x1, Pallas kernels, combine_call(): pl.pallas_call(combine_kernel, out_shape=jax.ShapeDtypeStruct((32, dim),...  22.1 us
    unnamed x5, local copies, waits for them, and re-layouts  4.2 us

profile of v6, /device:TPU:0, one launch (start us, length us, event | category | flops | bytes accessed | tf_op | source)
XLA Modules:
  0.0 123.1 jit_solution(15549074947226688762)
XLA Ops:
  0.6 28.0 %attend.1 = (bf16[256,128,128]{2,1,0:T(8,128)(2,1)}, bf16[256,128,128]{2,1,0:T(8,128)(2,1)}, f32[128,32,128]{2,1,0:T(8,128)}, f32[2,32,128]{2,1,0:T(8,128)}) custom-call(s32[256]{0:T(256)} %lens_ref.1, s32[256]{0:T(256)} %lens_ref.1, f32[1,128]{1,0:T(1,128)} %constant.2.clone.freq_ref, bf16[5120]{0:T(1024)(128)(2,1)} %g_ref.2, bf16[256,5120]{1,0:T(8,128)(2,1)} %x_hbm.3, ...), custom_call_target="tpu_custom_call" | custom-call | tf_op jit(solution)/shard_map/attend/pallas_call | solution.py:169
  28.6 22.1 %combine.1.part_hbm = f32[32,5120]{1,0:T(8,128)} custom-call(f32[128,32,128]{2,1,0:T(8,128)} %get-tuple-element.9.mix_hbm, f32[2,32,128]{2,1,0:T(8,128)} %get-tuple-element.10.st_own, bf16[2048,5120]{1,0:T(8,128)(2,1)} %wo.1), custom_call_target="tpu_custom_call" | custom-call | tf_op jit(solution)/shard_map/combine/pallas_call | solution.py:318
  50.8 32.8 %hidden.1 = (f32[128,5120]{1,0:T(8,128)}, f32[16,5120]{1,0:T(8,128)}) custom-call(f32[32,5120]{1,0:T(8,128)} %combine.1.part_hbm, bf16[256,5120]{1,0:T(8,128)(2,1)} %x_hbm.3, bf16[5120]{0:T(1024)(128)(2,1)} %g_ref.3, bf16[5120,7168]{1,0:T(8,128)(2,1)} %wg.1, bf16[5120,7168]{1,0:T(8,128)(2,1)} %wu.1, bf16[7168,5120]{1,0:T(8,128)(2,1)} %wd.1), custom_call_target="tpu_custom_call" | custom-call | tf_op jit(solution)/shard_map/hidden/pallas_call | solution.py:471
  83.5 0.0 copy-start
  83.5 1.7 %copy-done = f32[128,5120]{1,0:T(8,128)S(1)} copy-done((f32[128,5120]{1,0:T(8,128)S(1)}, f32[128,5120]{1,0:T(8,128)}, u32[]{:S(2)}) %copy-start) | copy-done | bytes 2621464
  85.3 0.0 copy-start.1
  85.3 1.0 copy-done.1
  86.2 35.4 %output.1 = bf16[256,5120]{1,0:T(8,128)(2,1)S(1)} custom-call(f32[128,5120]{1,0:T(8,128)S(1)} %copy-done, f32[16,5120]{1,0:T(8,128)S(1)} %copy-done.1), custom_call_target="tpu_custom_call" | custom-call | tf_op jit(solution)/shard_map/output/pallas_call | solution.py:593
  121.7 1.5 %copy.18 = bf16[256,5120]{1,0:T(8,128)(2,1)} copy(bf16[256,5120]{1,0:T(8,128)(2,1)S(1)} %output.1) | data formatting | bytes 5242880
Async XLA Ops:
  83.5 1.7 %copy-start = (f32[128,5120]{1,0:T(8,128)S(1)}, f32[128,5120]{1,0:T(8,128)}, u32[]{:S(2)}) copy-start(f32[128,5120]{1,0:T(8,128)} %get-tuple-element.11.part_ref) | copy-start | bytes 7864324
  85.3 1.0 copy-start.1
